TPU v7x, 16 devices: a whole 2x2x2 slice. The times are simulated.
16 devices in a mesh: dp: 2 (over z), ep: 8 (over y, x, core).
Axes of the slice: x: 2, y: 2, z: 2, core: 2. Of those that a mesh axis runs over, the one named last changes fastest.
Arguments:
- x_tokens: bfloat16 [2048, 1024], P(('dp', 'ep'))
- expert_idx: int32 [2048, 8], P(('dp', 'ep'))
- d_out: bfloat16 [2048, 1024], P(('dp', 'ep'))
- norm_w: bfloat16 [1024], replicated
- w_router: bfloat16 [1024, 32], replicated
- b_router: float32 [32], replicated
- w_gate_up: bfloat16 [32, 1024, 1024], P('ep')
- b_gate_up: float32 [32, 1024], P('ep')
- w_down: bfloat16 [32, 512, 1024], P('ep')
- b_down: float32 [32, 1024], P('ep')
Outputs:
- output 1: bfloat16 [2048, 1024], P(('dp', 'ep'))
- output 2: bfloat16 [2048, 1024], P(('dp', 'ep'))
- output 3: float32 [32, 1024, 1024], P('ep')
- output 4: float32 [32, 1024], P('ep')
- output 5: float32 [32, 512, 1024], P('ep')
- output 6: float32 [32, 1024], P('ep')
- output 7: float32 [1024, 32], replicated
- output 8: float32 [32], replicated
- output 9: float32 [1024], replicated
All inputs are finite; a program needn't handle non-finite values.
Results may differ from a plain program's by a relative error of at most 0.00492042.
Values are sent between devices in bfloat16 or wider.
A program may use at most 1 GiB of HBM per device.

v0:
```python
import jax
import jax.numpy as jnp
from jax import lax
from jax.sharding import PartitionSpec as P

SWIGLU_LIMIT = 7.0
SIG_ALPHA = 1.702
NORM_EPS = 1e-5


def norm_and_route(x_tokens, expert_idx, norm_w, w_router, b_router):
    x_float = x_tokens.astype(jnp.float32)
    inv_rms = lax.rsqrt(jnp.mean(x_float * x_float, axis=-1, keepdims=True) + NORM_EPS)
    normed = x_float * inv_rms
    h_bf = (normed * norm_w.astype(jnp.float32)).astype(jnp.bfloat16)
    logits = jnp.dot(h_bf, w_router, preferred_element_type=jnp.float32) + b_router
    route_prob = jax.nn.softmax(jnp.take_along_axis(logits, expert_idx, axis=1), axis=-1)
    return x_float, inv_rms, normed, h_bf, route_prob


def glu_parts(gate_up, width):
    gate_pre = gate_up[:, :width]
    up_pre = gate_up[:, width:]
    gate_c = jnp.minimum(gate_pre, SWIGLU_LIMIT)
    up_c = jnp.clip(up_pre, -SWIGLU_LIMIT, SWIGLU_LIMIT)
    sig_gate = jax.nn.sigmoid(SIG_ALPHA * gate_c)
    return gate_pre, up_pre, gate_c, up_c, sig_gate


def glu_forward(gate_up, width):
    gate_pre, up_pre, gate_c, up_c, sig_gate = glu_parts(gate_up, width)
    return (gate_c * sig_gate * (up_c + 1.0)).astype(jnp.bfloat16)


def glu_backward(d_act, gate_up, width):
    gate_pre, up_pre, gate_c, up_c, sig_gate = glu_parts(gate_up, width)
    d_gate = jnp.where(gate_pre < SWIGLU_LIMIT, d_act * (up_c + 1.0) * sig_gate * (1.0 + SIG_ALPHA * gate_c * (1.0 - sig_gate)), 0.0)
    d_up = jnp.where((up_pre > -SWIGLU_LIMIT) & (up_pre < SWIGLU_LIMIT), d_act * gate_c * sig_gate, 0.0)
    return jnp.concatenate([d_gate, d_up], axis=1)


def router_backward(pair_dot, route_prob, expert_idx, h_bf, w_router):
    n_experts = w_router.shape[1]
    d_sel = route_prob * (pair_dot - jnp.sum(route_prob * pair_dot, axis=1, keepdims=True))
    expert_hits = expert_idx[:, :, None] == jnp.arange(n_experts)[None, None, :]
    d_logits = jnp.sum(jnp.where(expert_hits, d_sel[:, :, None], 0.0), axis=1)
    dlog_bf = d_logits.astype(jnp.bfloat16)
    grad_router = lax.dot_general(h_bf, dlog_bf, (((0,), (0,)), ((), ())), preferred_element_type=jnp.float32)
    dh_router = lax.dot_general(dlog_bf, w_router, (((1,), (1,)), ((), ())), preferred_element_type=jnp.float32)
    return grad_router, jnp.sum(d_logits, axis=0), dh_router


def norm_backward(d_out, d_h, normed, inv_rms, norm_w):
    grad_norm = jnp.sum(d_h * normed, axis=0)
    d_normed = d_h * norm_w.astype(jnp.float32)
    d_x = d_out.astype(jnp.float32) + inv_rms * (d_normed - normed * jnp.mean(d_normed * normed, axis=-1, keepdims=True))
    return d_x.astype(jnp.bfloat16), grad_norm


def grouped_dot(left_op, right_op, group_sizes):
    dim_numbers = lax.RaggedDotDimensionNumbers(dot_dimension_numbers=(([1], [2]), ([], [])), lhs_ragged_dimensions=[0], rhs_group_dimensions=[0])
    return lax.ragged_dot_general(left_op, right_op, group_sizes, dim_numbers, preferred_element_type=jnp.float32)


def grouped_outer(left_op, right_op, group_sizes):
    dim_numbers = lax.RaggedDotDimensionNumbers(dot_dimension_numbers=(([0], [0]), ([], [])), lhs_ragged_dimensions=[0], rhs_group_dimensions=[])
    return lax.ragged_dot_general(left_op, right_op, group_sizes, dim_numbers, preferred_element_type=jnp.float32)


def solution(mesh):
    tok_spec = P("dp", None) if False else P(("dp", "ep"), None)
    rep_spec = P()

    def block_body(x_tokens, expert_idx, d_out, norm_w, w_router, b_router, w_gate_up, b_gate_up, w_down, b_down):
        n_local = w_gate_up.shape[0]
        width = w_down.shape[1]
        top_k = expert_idx.shape[1]
        my_ep = lax.axis_index("ep")
        x_float, inv_rms, normed, h_bf, route_prob = norm_and_route(x_tokens, expert_idx, norm_w, w_router, b_router)
        h_all = lax.all_gather(h_bf, "ep", axis=0, tiled=True)
        idx_all = lax.all_gather(expert_idx, "ep", axis=0, tiled=True)
        prob_all = lax.all_gather(route_prob, "ep", axis=0, tiled=True)
        n_all = h_all.shape[0]
        rel_ids = idx_all.reshape(-1) - my_ep * n_local
        is_local = (rel_ids >= 0) & (rel_ids < n_local)
        group_key = jnp.where(is_local, rel_ids, n_local)
        pair_order = jnp.argsort(group_key, stable=True)
        sorted_key = group_key[pair_order]
        group_sizes = jax.ops.segment_sum(jnp.ones_like(group_key), group_key, num_segments=n_local + 1)[:n_local]
        valid_pair = sorted_key < n_local
        valid_col = valid_pair[:, None]
        bias_key = jnp.minimum(sorted_key, n_local - 1)
        tok_of = pair_order // top_k
        pair_prob = jnp.where(valid_pair, prob_all.reshape(-1)[pair_order], 0.0)
        h_rows = h_all[tok_of]
        gate_up = jnp.where(valid_col, lax.ragged_dot(h_rows, w_gate_up, group_sizes, preferred_element_type=jnp.float32) + b_gate_up[bias_key], 0.0)
        act_bf = glu_forward(gate_up, width)
        y_pair = jnp.where(valid_col, lax.ragged_dot(act_bf, w_down, group_sizes, preferred_element_type=jnp.float32) + b_down[bias_key], 0.0)
        y_part = jax.ops.segment_sum(pair_prob[:, None] * y_pair, tok_of, num_segments=n_all)
        y_home = lax.psum_scatter(y_part, "ep", scatter_dimension=0, tiled=True)
        y_out = (x_float + y_home).astype(jnp.bfloat16)
        dy_all = lax.all_gather(d_out, "ep", axis=0, tiled=True)
        dy_rows = dy_all[tok_of].astype(jnp.float32)
        dot_sorted = jnp.sum(dy_rows * y_pair, axis=1)
        dot_part = jax.ops.segment_sum(dot_sorted, pair_order, num_segments=n_all * top_k).reshape(n_all, top_k)
        v_pair = pair_prob[:, None] * dy_rows
        v_bf = v_pair.astype(jnp.bfloat16)
        grad_down = grouped_outer(act_bf, v_bf, group_sizes)
        grad_b_down = jax.ops.segment_sum(v_pair, sorted_key, num_segments=n_local + 1)[:n_local]
        d_act = jnp.where(valid_col, grouped_dot(v_bf, w_down, group_sizes), 0.0)
        d_gu = glu_backward(d_act, gate_up, width)
        d_gu_bf = d_gu.astype(jnp.bfloat16)
        grad_gate_up = grouped_outer(h_rows, d_gu_bf, group_sizes)
        grad_b_gate_up = jax.ops.segment_sum(d_gu, sorted_key, num_segments=n_local + 1)[:n_local]
        dh_rows = jnp.where(valid_col, grouped_dot(d_gu_bf, w_gate_up, group_sizes), 0.0)
        dh_part = jax.ops.segment_sum(dh_rows, tok_of, num_segments=n_all)
        dot_home = lax.psum_scatter(dot_part, "ep", scatter_dimension=0, tiled=True)
        dh_home = lax.psum_scatter(dh_part, "ep", scatter_dimension=0, tiled=True)
        grad_gate_up = lax.psum(grad_gate_up, "dp")
        grad_b_gate_up = lax.psum(grad_b_gate_up, "dp")
        grad_down = lax.psum(grad_down, "dp")
        grad_b_down = lax.psum(grad_b_down, "dp")
        grad_router, grad_b_router, dh_router = router_backward(dot_home, route_prob, expert_idx, h_bf, w_router)
        d_tokens, grad_norm = norm_backward(d_out, dh_home + dh_router, normed, inv_rms, norm_w)
        grad_router = lax.psum(grad_router, ("dp", "ep"))
        grad_b_router = lax.psum(grad_b_router, ("dp", "ep"))
        grad_norm = lax.psum(grad_norm, ("dp", "ep"))
        return (y_out, d_tokens, grad_gate_up, grad_b_gate_up, grad_down, grad_b_down, grad_router, grad_b_router, grad_norm)

    in_specs = (tok_spec, tok_spec, tok_spec, rep_spec, rep_spec, rep_spec, P("ep", None, None), P("ep", None), P("ep", None, None), P("ep", None))
    out_specs = (tok_spec, tok_spec, P("ep", None, None), P("ep", None), P("ep", None, None), P("ep", None), rep_spec, rep_spec, rep_spec)
    return jax.shard_map(block_body, mesh=mesh, in_specs=in_specs, out_specs=out_specs, check_vma=False)
```

profile of v0, /device:TPU:0, one launch (start us, length us, event | category | flops | bytes accessed | tf_op | source)
XLA Modules:
  0.0 1481.1 jit_solution(4262732304085737488)
XLA Ops:
  32.1 45.5 %gather_fusion = s32[8192]{0:T(1024)S(1)} fusion(s32[8192]{0:T(1024)S(1)} %and_select_fusion.1, s32[8192]{0:T(1024)S(1)} %get-tuple-element.52), kind=kCustom, calls=%fused_computation | custom fusion | bytes 98304 | tf_op jit(solution)/shard_map/gather | solution.py:88
  86.6 57.5 %scatter_custom_fusion = s32[5]{0:T(128)} fusion(s32[8192]{0:T(1024)S(1)} %bitcast.20, s32[8192]{0:T(1024)S(1)} %ne.14, s32[]{:T(128)} %constant.23.clone.1), kind=kCustom, calls=%fused_computation.95 | custom fusion | flops 8192 | bytes 24 | tf_op jit(solution)/shard_map/scatter-add | solution.py:89
  145.7 35.8 %gather_fusion.4 = f32[8192,1024]{1,0:T(8,128)} fusion(f32[4,1024]{1,0:T(4,128)S(1)} %copy-done.1, s32[8192]{0:T(1024)S(1)} %broadcast_clamp_fusion), kind=kCustom, calls=%fused_computation.4 | custom fusion | bytes 67141632 | tf_op jit(solution)/shard_map/gather | solution.py:98
  181.5 35.4 %gather_fusion.3 = f32[8192,1024]{1,0:T(8,128)} fusion(f32[4,1024]{1,0:T(4,128)S(1)} %copy-done.2, s32[8192]{0:T(1024)S(1)} %broadcast_clamp_fusion), kind=kCustom, calls=%fused_computation.3 | custom fusion | bytes 67141632 | tf_op jit(solution)/shard_map/gather | solution.py:96
  216.9 42.3 %gather_fusion.2 = bf16[8192,1024]{1,0:T(8,128)(2,1)} fusion(bf16[1024,1024]{1,0:T(8,128)(2,1)} %all-gather.3.cloned.1.call-done, s32[8192]{0:T(1024)S(1)} %copy-done.11), kind=kCustom, calls=%fused_computation.2 | custom fusion | bytes 33587200 | tf_op jit(solution)/shard_map/gather | solution.py:95
  259.3 13.4 ragged-dot-none.5
  272.7 33.4 %add_select_fusion.1 = f32[8192,1024]{1,0:T(8,128)} fusion(f32[8192,1024]{1,0:T(8,128)} %ragged-dot-none.5, f32[8192,1024]{1,0:T(8,128)} %gather_fusion.3, pred[8192]{0:T(1024)(128)(4,1)S(1)} %copy-done.14), kind=kLoop, calls=%fused_computation.24 | loop fusion | flops 16777216 | bytes 100671488 | tf_op jit(solution)/shard_map/jit(_where)/select_n | solution.py:96
  306.1 15.3 %multiply_convert_fusion = bf16[8192,512]{1,0:T(8,128)(2,1)} fusion(f32[8192,1024]{1,0:T(8,128)} %add_select_fusion.1), kind=kLoop, calls=%fused_computation.29 | loop fusion | flops 41943040 | bytes 41943040 | tf_op jit(solution)/shard_map/convert_element_type | solution.py:32
  332.2 42.5 %gather_fusion.5 = bf16[8192,1024]{1,0:T(8,128)(2,1)} fusion(bf16[1024,1024]{1,0:T(8,128)(2,1)} %all-gather.5.cloned.1.call-done, s32[8192]{0:T(1024)S(1)} %copy-done.11), kind=kCustom, calls=%fused_computation.5 | custom fusion | bytes 33587200 | tf_op jit(solution)/shard_map/gather | solution.py:103
  374.7 26.3 %fusion.2 = f32[8192]{0:T(1024)S(1)} fusion(bf16[8192,1024]{1,0:T(8,128)(2,1)} %gather_fusion.5, f32[8192,1024]{1,0:T(8,128)} %ragged-dot-none.4, f32[8192,1024]{1,0:T(8,128)} %gather_fusion.4, pred[8192]{0:T(1024)(128)(4,1)S(1)} %copy-done.14), kind=kLoop, calls=%fused_computation.17 | loop fusion | flops 41934848 | bytes 83927040 | tf_op jit(solution)/shard_map/reduce_sum | solution.py:104
  401.0 57.1 %scatter_custom_fusion.3 = f32[8192]{0:T(1024)S(1)} fusion(s32[8192]{0:T(1024)} %copy-done.22, f32[8192]{0:T(1024)S(1)} %fusion.2, f32[]{:T(128)} %constant.20.clone.1), kind=kCustom, calls=%fused_computation.77 | custom fusion | flops 8192 | bytes 33280 | tf_op jit(solution)/shard_map/scatter-add | solution.py:105
  498.4 45.5 %gather_fusion.1 = f32[8192]{0:T(1024)S(1)} fusion(f32[8192]{0:T(1024)S(1)} %reshape.104, s32[8192]{0:T(1024)S(1)} %copy-done.13), kind=kCustom, calls=%fused_computation.1 | custom fusion | bytes 98304 | tf_op jit(solution)/shard_map/gather | solution.py:94
  544.0 14.6 fusion.1
  569.0 28.9 %multiply_select_fusion.1 = (f32[8192,512]{1,0:T(8,128)S(1)}, f32[8192,512]{1,0:T(8,128)}) fusion(f32[8192,1024]{1,0:T(8,128)} %add_select_fusion.1, f32[8192,512]{1,0:T(8,128)} %ragged-dot-none.3, pred[8192]{0:T(1024)(128)(4,1)S(1)} %copy-done.14), kind=kLoop, calls=%fused_computation.28 | loop fusion | flops 92274688 | bytes 83894272 | tf_op jit(solution)/shard_map/jit(_where)/select_n | solution.py:37
  597.8 19.3 %fusion.8 = bf16[8192,1024]{1,0:T(8,128)(2,1)} fusion(f32[8192,512]{1,0:T(8,128)} %get-tuple-element.48, f32[8192,512]{1,0:T(8,128)S(1)} %get-tuple-element.47), kind=kLoop, calls=%fused_computation.26 | loop fusion | flops 33554432 | bytes 50331648 | tf_op jit(solution)/shard_map/convert_element_type | solution.py:112
  617.1 13.6 ragged-dot-none.2
  630.7 74.1 %scatter_custom_fusion.2 = f32[1024,1024]{1,0:T(8,128)} fusion(s32[8192]{0:T(1024)} %get-tuple-element.53, f32[8192,1024]{1,0:T(8,128)} %ragged-dot-none.2, f32[]{:T(128)} %constant.20.clone.1, pred[8192]{0:T(1024)(128)(4,1)S(1)} %copy-done.14), kind=kCustom, calls=%fused_computation.19 | custom fusion | flops 16777216 | bytes 37757952 | tf_op jit(solution)/shard_map/scatter-add | solution.py:116
  704.9 75.9 %scatter_custom_fusion.1 = f32[1024,1024]{1,0:T(8,128)} fusion(s32[8192]{0:T(1024)} %get-tuple-element.53, f32[8192]{0:T(1024)S(1)} %broadcast_select_fusion, f32[8192,1024]{1,0:T(8,128)} %ragged-dot-none.4, f32[8192,1024]{1,0:T(8,128)} %gather_fusion.4, f32[]{:T(128)} %constant.20.clone.1, pred[8192]{0:T(1024)(128)(4,1)S(1)} %copy-done.14), kind=kCustom, calls=%fused_computation.21 | custom fusion | flops 33554432 | bytes 71345152 | tf_op jit(solution)/shard_map/scatter-add | solution.py:99
  783.5 16.7 %ragged-dot-none.1 = f32[4,1024,1024]{2,1,0:T(8,128)} custom-call(s32[1]{0:T(128)} %get-tuple-element.15, s32[5]{0:T(128)} %get-tuple-element.16, s32[35]{0:T(128)} %get-tuple-element.17, s32[35]{0:T(128)} %get-tuple-element.18, s32[1]{0:T(128)} %get-tuple-element.15, bf16[8192,1024]{1,0:T(8,128)(2,1)} %gather_fusion.2, bf16[8192,1024]{1,0:T(8,128)(2,1)} %fusion.8), custom_call_target="tpu_custom_call" | custom-call | flops 17179869184 | bytes 50331664 | tf_op jit(solution)/shard_map/ragged_dot_general/ragged-dot-none
  800.1 13.1 ragged-dot-none
  813.3 70.7 %scatter_custom_fusion.5 = f32[5,1024]{1,0:T(8,128)S(1)} fusion(s32[8192]{0:T(1024)S(1)} %copy-done.10, bf16[8192,1024]{1,0:T(8,128)(2,1)} %gather_fusion.5, f32[8192]{0:T(1024)S(1)} %broadcast_select_fusion, f32[]{:T(128)} %constant.20.clone.1), kind=kCustom, calls=%fused_computation.15 | custom fusion | flops 25165824 | bytes 16830468 | tf_op jit(solution)/shard_map/scatter-add | solution.py:109
  884.0 68.9 %scatter_custom_fusion.4 = f32[5,1024]{1,0:T(8,128)S(1)} fusion(s32[8192]{0:T(1024)S(1)} %copy-done.10, f32[8192,512]{1,0:T(8,128)} %get-tuple-element.48, f32[]{:T(128)} %constant.37.clone.1, f32[8192,512]{1,0:T(8,128)} %copy-done.3, f32[]{:T(128)} %constant.20.clone.1), kind=kCustom, calls=%fused_computation.25 | custom fusion | flops 16777216 | bytes 33574920 | tf_op jit(solution)/shard_map/scatter-add | solution.py:114
  964.0 35.2 %all-reduce = (f32[32]{0:T(128)}, f32[1024]{0:T(1024)}) all-reduce(f32[32]{0:T(128)S(1)} %get-tuple-element.37, f32[1024]{0:T(1024)S(1)} %get-tuple-element.35), channel_id=1, replica_groups=mesh['dp'=2,'ep'=8] {'dp','ep'}, use_global_device_ids=true, to_apply=%region_23.24 | all-reduce | flops 1056 | bytes 8448 | tf_op jit(solution)/shard_map/psum | solution.py:126
  1001.4 454.4 %all-reduce.8.cloned.1.call-done = (f32[4,1024,1024]{2,1,0:T(8,128)}, f32[4,512,1024]{2,1,0:T(8,128)}) async-done(((f32[4,1024,1024]{2,1,0:T(8,128)}, f32[4,512,1024]{2,1,0:T(8,128)}), (f32[4,1024,1024]{2,1,0:T(8,128)}, f32[4,512,1024]{2,1,0:T(8,128)})) %all-reduce.8.cloned.1.call-update) | async-done | bytes 25165840 | tf_op jit(solution)/shard_map/psum | solution.py:119
  (129 shorter events, 130.8 us)
Async XLA Ops:
  7.2 71.3 %copy-start = (bf16[1024,32]{0,1:T(8,128)(2,1)S(1)}, bf16[1024,32]{0,1:T(8,128)(2,1)}, u32[]{:S(2)}) copy-start(bf16[1024,32]{0,1:T(8,128)(2,1)} %param.14) | copy-start | bytes 196612
  7.2 209.8 %all-gather.3.cloned.1.call-start = ((), (), s32[]{:S(2)}) async-start(), calls=%async_computation.3 | async-start | bytes 2359296 | tf_op jit(solution)/shard_map/all_gather | solution.py:80
  11.4 320.8 %all-gather.5.cloned.1.call-start = ((), (), s32[]{:S(2)}) async-start(), calls=%async_computation.5 | async-start | bytes 2359296 | tf_op jit(solution)/shard_map/all_gather | solution.py:102
  12.2 476.1 %reduce-scatter.8.cloned.1.call-start = ((), (), s32[]{:S(2)}) async-start(), calls=%async_computation.7 | async-start | bytes 36864 | tf_op jit(solution)/shard_map/reduce_scatter | solution.py:117
  31.5 46.2 %copy-start.22 = (s32[8192]{0:T(1024)}, s32[8192]{0:T(1024)S(1)}, u32[]{:S(2)}) copy-start(s32[8192]{0:T(1024)S(1)} %get-tuple-element.10) | copy-start | bytes 98308
  32.1 46.4 %copy-start.5 = (bf16[128,1024]{1,0:T(8,128)(2,1)S(1)}, bf16[128,1024]{1,0:T(8,128)(2,1)}, u32[]{:S(2)}) copy-start(bf16[128,1024]{1,0:T(8,128)(2,1)} %fusion.19) | copy-start | bytes 786436
  32.1 46.4 %copy-start.27 = (f32[32]{0:T(128)S(1)}, f32[32]{0:T(128)}, u32[]{:S(2)}) copy-start(f32[32]{0:T(128)} %param.15) | copy-start | bytes 388
  85.8 59.9 %copy-start.1 = (f32[4,1024]{1,0:T(4,128)S(1)}, f32[4,1024]{1,0:T(4,128)}, u32[]{:S(2)}) copy-start(f32[4,1024]{1,0:T(4,128)} %param.19) | copy-start | bytes 49156
  85.9 59.8 %copy-start.20 = (f32[128,8]{0,1:T(8,128)}, f32[128,8]{0,1:T(8,128)S(1)}, u32[]{:S(2)}) copy-start(f32[128,8]{0,1:T(8,128)S(1)} %copy.45) | copy-start | bytes 12292
  374.7 84.6 %copy-start.16 = (s32[128,8]{0,1:T(8,128)S(1)}, s32[128,8]{0,1:T(8,128)}, u32[]{:S(2)}) copy-start(s32[128,8]{0,1:T(8,128)} %param.11) | copy-start | bytes 12292
  374.7 84.6 %copy-start.21 = (f32[128,8]{0,1:T(8,128)S(1)}, f32[128,8]{0,1:T(8,128)}, u32[]{:S(2)}) copy-start(f32[128,8]{0,1:T(8,128)} %copy-done.20) | copy-start | bytes 12292
  374.7 84.6 %copy-start.24 = (f32[128]{0:T(128)S(1)}, f32[128]{0:T(128)}, u32[]{:S(2)}) copy-start(f32[128]{0:T(128)} %fusion.43) | copy-start | bytes 1540
  401.0 97.4 %copy-start.13 = (s32[8192]{0:T(1024)S(1)}, s32[8192]{0:T(1024)}, u32[]{:S(2)}) copy-start(s32[8192]{0:T(1024)} %copy-done.12) | copy-start | bytes 98308
  459.2 503.4 %reduce-scatter.6.cloned.1.call-start = ((), (), s32[]{:S(2)}) async-start(), calls=%async_computation.6 | async-start | bytes 4718592 | tf_op jit(solution)/shard_map/reduce_scatter | solution.py:118
  498.4 45.6 %copy-start.10 = (s32[8192]{0:T(1024)S(1)}, s32[8192]{0:T(1024)}, u32[]{:S(2)}) copy-start(s32[8192]{0:T(1024)} %copy-done.9) | copy-start | bytes 98308
  704.8 77.6 %copy-start.23 = (f32[128,8]{0,1:T(8,128)S(1)}, f32[128,8]{0,1:T(8,128)}, u32[]{:S(2)}) copy-start(f32[128,8]{0,1:T(8,128)} %reduce-scatter.8.cloned.1.call-done) | copy-start | bytes 12292
  704.9 77.7 %copy-start.6 = (bf16[128,1024]{1,0:T(8,128)(2,1)S(1)}, bf16[128,1024]{1,0:T(8,128)(2,1)}, u32[]{:S(2)}) copy-start(bf16[128,1024]{1,0:T(8,128)(2,1)} %fusion.19) | copy-start | bytes 786436
  704.9 294.4 %reduce-scatter.4.cloned.1.call-start = ((), (), s32[]{:S(2)}) async-start(), calls=%async_computation.4 | async-start | bytes 4718592 | tf_op jit(solution)/shard_map/reduce_scatter | solution.py:100
  780.8 220.6 %all-reduce.6.cloned.1.call-start = ((), (), s32[]{:S(2)}) async-start(), calls=%async_computation.8 | async-start | bytes 262144 | tf_op jit(solution)/shard_map/psum | solution.py:125
  783.4 672.3 %all-reduce.8.cloned.1.call-start = ((), (), s32[]{:S(2)}) async-start(), calls=%async_computation.9 | async-start | bytes 50331648 | tf_op jit(solution)/shard_map/psum | solution.py:119
  884.0 78.6 %copy-start.7 = (bf16[128,1024]{1,0:T(8,128)(2,1)S(1)}, bf16[128,1024]{1,0:T(8,128)(2,1)}, u32[]{:S(2)}) copy-start(bf16[128,1024]{1,0:T(8,128)(2,1)} %param.10) | copy-start | bytes 786436
  884.0 78.6 %copy-start.19 = (f32[1024]{0:T(1024)S(1)}, f32[1024]{0:T(1024)}, u32[]{:S(2)}) copy-start(f32[1024]{0:T(1024)} %copy-done.18) | copy-start | bytes 12292
  884.0 78.6 %copy-start.26 = (f32[128]{0:T(128)S(1)}, f32[128]{0:T(128)}, u32[]{:S(2)}) copy-start(f32[128]{0:T(128)} %copy-done.25) | copy-start | bytes 1540
  884.0 115.3 %copy-start.8 = (bf16[128,1024]{1,0:T(8,128)(2,1)S(1)}, bf16[128,1024]{1,0:T(8,128)(2,1)}, u32[]{:S(2)}) copy-start(bf16[128,1024]{1,0:T(8,128)(2,1)} %param.12) | copy-start | bytes 786436
  (11 other events, 183.5 us)
Sparse Core Ops, SparseCore 0:
  11.5 28.4 all-gather.2
  41.9 23.7 all-gather.4
  459.3 28.9 reduce-scatter.7
  705.0 47.2 reduce-scatter.5
  780.9 47.2 reduce-scatter.3
  832.9 65.0 all-reduce.5
  901.1 554.5 all-reduce.7
where the time goes:
time: 1490 us; the launch traced here: 1480 us
  other arithmetic  558 us (37%)
  waiting for transfers between devices  467 us (31%)
  local copies, waits for them, and re-layouts  293 us (20%)
  Pallas kernels  81.1 us (5%)
  blocking collectives  64.7 us (4%)
  between operations  15 us (1%)
    psum x1, waiting for transfers between devices, block_body(): grad_gate_up = lax.psum(grad_gate_up, 'dp')  454 us
    scatter-add x1, other arithmetic, block_body(): jax.ops.segment_sum(pair_prob[:, None] * y_pair, tok_of, num_segments=n_all)  75.9 us
    scatter-add x1, other arithmetic, block_body(): dh_part = jax.ops.segment_sum(dh_rows, tok_of, num_segments=n_all)  74.1 us
    scatter-add x1, other arithmetic, block_body(): jax.ops.segment_sum(v_pair, sorted_key, num_segments=n_local + 1)[:n_local]  70.7 us
    scatter-add x1, other arithmetic, block_body(): jax.ops.segment_sum(d_gu, sorted_key, num_segments=n_local + 1)[:n_local]  68.9 us
    scatter-add x1, other arithmetic, block_body(): jax.ops.segment_sum(jnp.ones_like(group_key), group_key, num_segments=n_l...  57.5 us
    scatter-add x1, other arithmetic, block_body(): jax.ops.segment_sum(dot_sorted, pair_order, num_segments=n_all * top_k)  57.1 us
    another operation x4, Pallas kernels  54 us
  transfers between devices with their start and end apart: 7, of which 2 were waited for; matrix products, arithmetic and copies ran while one was open for 35% of the time, Pallas kernels for 4%

commit v1 on v0

v1 whole, which is shorter than its diff:
```python
import functools

import jax
import jax.numpy as jnp
from jax import lax
from jax.experimental import pallas as pl
from jax.experimental.pallas import tpu as pltpu
from jax.sharding import PartitionSpec as P

SWIGLU_LIMIT = 7.0
SIG_ALPHA = 1.702
NORM_EPS = 1e-5
F32 = jnp.float32
BF16 = jnp.bfloat16
MESH = pl.DeviceIdType.MESH
NT = (((1,), (1,)), ((), ()))
D = 1024
F = 512
E = 32
EL = 4
T = 128
WR = 2 * D + 128
ROWS = 32
COLS = 256


def block_kernel(x_ref, idx_ref, dout_ref, nw_ref, wr_ref, br_ref, wgu_hbm, bgu_ref, wdn_hbm, bdn_ref,
                 y_out, dt_out, gbgu_ref, gbdn_ref, g_out, h_hbm, a_hbm, c_hbm, v_hbm,
                 hd, pt, ph, pb, wgu, wdn, gu, da, a_st, c_st, v_st, yt, part, rd, rr, gath, accg, accd,
                 ag_s, ag_r, pt_s, pt_r, d2d_s, d2d_r, rs_s, rs_r, g_s, g_r, w_sem, st_sem, h_sem):
    d = lax.axis_index("dp")
    e = lax.axis_index("ep")
    k = e % 2
    cx = (e // 2) % 2
    cy = e // 4

    def chip(m):
        return ((cy + m // 2) % 2) * 2 + (cx + m % 2) % 2

    def ep_of(m, kk):
        return chip(m) * 2 + kk

    def dev(r):
        kk = (k + r % 2) % 2
        xx = (cx + (r // 2) % 2) % 2
        yy = (cy + (r // 4) % 2) % 2
        return ((d + r // 8) % 2, (yy * 2 + xx) * 2 + kk)

    sib = (d, e + 1 - 2 * k)
    zp = (1 - d, e)
    me = d * 8 + e

    for j in range(EL):
        pltpu.make_async_copy(wgu_hbm.at[j], wgu.at[j], w_sem.at[0, j]).start()
        pltpu.make_async_copy(wdn_hbm.at[j], wdn.at[j], w_sem.at[1, j]).start()

    barrier = pltpu.get_barrier_semaphore()

    @pl.loop(1, 16)
    def _(r):
        pl.semaphore_signal(barrier, inc=1, device_id=dev(r), device_id_type=MESH)

    x = x_ref[...].astype(F32)
    inv = lax.rsqrt(jnp.mean(x * x, axis=-1, keepdims=True) + NORM_EPS)
    normed = x * inv
    h = (normed * nw_ref[...].astype(F32)).astype(BF16)
    hd[me, :, :D] = h
    hd[me, :, D:] = dout_ref[...]
    logits = jnp.dot(h, wr_ref[...], preferred_element_type=F32) + br_ref[...]
    idx = idx_ref[...]
    lane = lax.broadcasted_iota(jnp.int32, (T, E), 1)
    hit = idx[:, 0:1] == lane
    for i in range(1, 8):
        hit = hit | (idx[:, i:i + 1] == lane)
    top = jnp.max(jnp.where(hit, logits, -jnp.inf), axis=-1, keepdims=True)
    ex = jnp.where(hit, jnp.exp(logits - top), 0.0)
    prob = ex / jnp.sum(ex, axis=-1, keepdims=True)
    ph[...] = prob
    pt[me] = prob.T

    pl.semaphore_wait(barrier, 15)

    def ag(i, g, to):
        return (pltpu.make_async_remote_copy(hd.at[g], hd.at[g], ag_s.at[i], ag_r.at[i], device_id=to, device_id_type=MESH),
                pltpu.make_async_remote_copy(pt.at[g], pt.at[g], pt_s.at[i], pt_r.at[i], device_id=to, device_id_type=MESH))

    def ag_send(i, g, to):
        for cp in ag(i, g, to):
            cp.start()

    def ag_wait(i, g):
        for cp in ag(i, g, sib):
            cp.wait_recv()

    ag_send(7, me, sib)
    ag_send(0, me, (d, ep_of(1, k)))
    ag_send(1, me, (d, ep_of(2, k)))
    ag_send(3, me, zp)
    ag_send(2, me, (d, ep_of(3, k)))

    accg[...] = jnp.zeros_like(accg)
    accd[...] = jnp.zeros_like(accd)

    def rd_copy(m):
        return pltpu.make_async_remote_copy(part.at[m, 1 - k], rd.at[m], d2d_s.at[m], d2d_r.at[m], device_id=sib, device_id_type=MESH)

    def rs_copy(m):
        return pltpu.make_async_remote_copy(part.at[m, k], rr.at[m - 1], rs_s.at[m - 1], rs_r.at[m - 1], device_id=(d, ep_of(m, k)), device_id_type=MESH)

    def st_copies(par, j, slot):
        return (pltpu.make_async_copy(a_st.at[par], a_hbm.at[j, pl.ds(slot * T, 2 * T)], st_sem.at[0, par]),
                pltpu.make_async_copy(c_st.at[par], c_hbm.at[j, pl.ds(slot * T, 2 * T)], st_sem.at[1, par]),
                pltpu.make_async_copy(v_st.at[par], v_hbm.at[j, pl.ds(slot * T, 2 * T)], st_sem.at[2, par]))

    def h_copy(slot):
        return pltpu.make_async_copy(hd.at[pl.ds(slot, 2), :, pl.ds(0, D)], h_hbm.at[pl.ds(slot, 2)], h_sem)

    def stage_probs(slot):
        sub = lax.broadcasted_iota(jnp.int32, (E, T), 0)
        for cc in range(2):
            rows = pt[slot + cc]
            for j in range(EL):
                row = jnp.sum(jnp.where(sub == 4 * e + j, rows, 0.0), axis=0, keepdims=True)
                pb[j, cc * T:(cc + 1) * T, :] = jnp.broadcast_to(row, (T, T)).T

    def expert(m, j, slot, own):
        par = j % 2
        hx = hd[pl.ds(slot, 2), :, :D].reshape(2 * T, D)
        gu[...] = jnp.dot(hx, wgu[j], preferred_element_type=F32)
        for r in range(0, 2 * T, ROWS):
            p = pb[j, r:r + ROWS, :]
            acc = None
            for c in range(0, D, COLS):
                dy = hd[slot + r // T, r % T:r % T + ROWS, D + c:D + c + COLS].astype(F32)
                v = jnp.concatenate([p] * (COLS // 128), axis=1) * dy
                v_st[par, r:r + ROWS, c:c + COLS] = v.astype(BF16)
                accd[j, :, c:c + COLS] += jnp.sum(v.reshape(ROWS // 8, 8, COLS), axis=0)
        da[...] = lax.dot_general(v_st[par], wdn[j], NT, preferred_element_type=F32)
        for r in range(0, 2 * T, ROWS):
            for c in range(0, F, COLS):
                gpre = gu[r:r + ROWS, c:c + COLS] + bgu_ref[j, :, c:c + COLS]
                upre = gu[r:r + ROWS, F + c:F + c + COLS] + bgu_ref[j, :, F + c:F + c + COLS]
                gc = jnp.minimum(gpre, SWIGLU_LIMIT)
                uc = jnp.clip(upre, -SWIGLU_LIMIT, SWIGLU_LIMIT)
                sg = jax.nn.sigmoid(SIG_ALPHA * gc)
                gs = gc * sg
                u1 = uc + 1.0
                a_st[par, r:r + ROWS, c:c + COLS] = (gs * u1).astype(BF16)
                dact = da[r:r + ROWS, c:c + COLS]
                dg = jnp.where(gpre < SWIGLU_LIMIT, dact * u1 * sg * (1.0 + SIG_ALPHA * gc * (1.0 - sg)), 0.0)
                du = jnp.where((upre > -SWIGLU_LIMIT) & (upre < SWIGLU_LIMIT), dact * gs, 0.0)
                c_st[par, r:r + ROWS, c:c + COLS] = dg.astype(BF16)
                c_st[par, r:r + ROWS, F + c:F + c + COLS] = du.astype(BF16)
                accg[j, :, c:c + COLS] += jnp.sum(dg.reshape(ROWS // 8, 8, COLS), axis=0)
                accg[j, :, F + c:F + c + COLS] += jnp.sum(du.reshape(ROWS // 8, 8, COLS), axis=0)
        if own:
            yt[...] = jnp.dot(a_st[par], wdn[j], preferred_element_type=F32)
            gu[...] = lax.dot_general(c_st[par], wgu[j], NT, preferred_element_type=F32)
            lanes = lax.broadcasted_iota(jnp.int32, (ROWS, 128), 1)
            for r in range(0, 2 * T, ROWS):
                p = pb[j, r:r + ROWS, :]
                cc, rt = r // T, r % T
                acc = jnp.zeros((ROWS, 128), F32)
                for c in range(0, D, 128):
                    yv = yt[r:r + ROWS, c:c + 128] + bdn_ref[j, :, c:c + 128]
                    dy = hd[slot + cc, rt:rt + ROWS, D + c:D + c + 128].astype(F32)
                    acc = acc + dy * yv
                    part[m, cc, rt:rt + ROWS, c:c + 128] += p * yv
                    part[m, cc, rt:rt + ROWS, D + c:D + c + 128] += gu[r:r + ROWS, c:c + 128]
                q = jnp.sum(acc, axis=1, keepdims=True)
                part[m, cc, rt:rt + ROWS, 2 * D:] += jnp.where(lanes == 4 * e + j, q, 0.0)

    def pre_expert(s, j, first):
        par = j % 2

        @pl.when(s * EL + j >= first)
        def _():
            for cp in st_copies(par, j, 0):
                cp.wait()

    @pl.loop(0, 4)
    def _(m):
        slot = d * 8 + chip(m) * 2
        ag_wait(7 + m, 0)
        h_copy(slot).start()
        stage_probs(slot)
        part[m] = jnp.zeros((2, T, WR), F32)

        @pl.loop(0, EL)
        def _(j):
            @pl.when(m == 0)
            def _():
                pltpu.make_async_copy(wgu_hbm.at[j], wgu.at[j], w_sem.at[0, j]).wait()
                pltpu.make_async_copy(wdn_hbm.at[j], wdn.at[j], w_sem.at[1, j]).wait()

            pre_expert(m, j, 2)
            expert(m, j, slot, True)
            for cp in st_copies(j % 2, j, slot):
                cp.start()

            @pl.when((j == 0) & (m >= 1))
            def _():
                rd_copy(m - 1).start()

            @pl.when((j == 1) & (m >= 1))
            def _():
                rd_copy(m - 1).wait_recv()
                part[m - 1, k] += rd[m - 1]

            @pl.when((j == 2) & (m >= 2))
            def _():
                rs_copy(m - 1).start()

            @pl.when((j == EL - 1) & (m < 3))
            def _():
                ag_wait(m, 0)
                g = d * 8 + ep_of(m + 1, k)
                ag_send(8 + m, g, sib)
                ag_send(4 + m, g, zp)

            @pl.when((j == EL - 1) & (m == 3))
            def _():
                ag_wait(3, 0)
                ag_send(11, (1 - d) * 8 + e, sib)

        h_copy(slot).wait()

    @pl.loop(0, 4)
    def _(m):
        slot = (1 - d) * 8 + chip(m) * 2
        ag_wait(11 + m, 0)
        h_copy(slot).start()
        stage_probs(slot)

        @pl.loop(0, EL)
        def _(j):
            pre_expert(m, j, 0)
            expert(m, j, slot, False)
            for cp in st_copies(j % 2, j, slot):
                cp.start()

            @pl.when((j == 0) & (m == 0))
            def _():
                rd_copy(3).start()

            @pl.when((j == 1) & (m == 0))
            def _():
                rd_copy(3).wait_recv()
                part[3, k] += rd[3]

            @pl.when((j == 2) & (m == 0))
            def _():
                rs_copy(3).start()

            @pl.when((j == EL - 1) & (m < 3))
            def _():
                ag_wait(4 + m, 0)
                ag_send(12 + m, (1 - d) * 8 + ep_of(m + 1, k), sib)

        h_copy(slot).wait()

    for par in range(2):
        for cp in st_copies(par, 0, 0):
            cp.wait()
    for j in range(EL):
        gbgu_ref[j] = jnp.sum(accg[j], axis=0, keepdims=True)
        gbdn_ref[j] = jnp.sum(accd[j], axis=0, keepdims=True)

    for m in range(1, 4):
        rs_copy(m).wait_recv()
    x = x_ref[...].astype(F32)
    inv = lax.rsqrt(jnp.mean(x * x, axis=-1, keepdims=True) + NORM_EPS)
    normed = x * inv
    tot = part[0, k] + rr[0] + rr[1] + rr[2]
    y_out[...] = (x + tot[:, :D]).astype(BF16)
    prob = ph[...]
    q = tot[:, 2 * D:2 * D + E]
    dlog = prob * (q - jnp.sum(prob * q, axis=1, keepdims=True))
    d_h = tot[:, D:2 * D] + lax.dot_general(dlog.astype(BF16), wr_ref[...], NT, preferred_element_type=F32)
    gath[me, :E, :] = dlog.T
    gn = jnp.sum(d_h * normed, axis=0, keepdims=True)
    for i in range(8):
        gath[me, E + i:E + i + 1, :] = gn[:, i * 128:(i + 1) * 128]
    dn = d_h * nw_ref[...].astype(F32)
    dt_out[...] = (dout_ref[...].astype(F32) + inv * (dn - normed * jnp.mean(dn * normed, axis=-1, keepdims=True))).astype(BF16)

    def g_copy(r):
        return pltpu.make_async_remote_copy(gath.at[me], gath.at[me], g_s.at[r], g_r.at[r], device_id=dev(r), device_id_type=MESH)

    @pl.loop(1, 16)
    def _(r):
        g_copy(r).start()

    for i in range(15):
        for cp in ag(i, 0, sib):
            cp.wait_send()
    for m in range(4):
        rd_copy(m).wait_send()
    for m in range(1, 4):
        rs_copy(m).wait_send()

    @pl.loop(1, 16)
    def _(r):
        g_copy(r).wait()

    g_out[...] = gath[...]


def grads_kernel(h_ref, a_ref, c_ref, v_ref, g_ref, ggu_ref, gdn_ref, gr_ref, gbr_ref, gn_ref, ht, at, dl):
    first = (pl.program_id(0) == 0) & (pl.program_id(1) == 0)

    @pl.when(first)
    def _():
        gbr = jnp.zeros((E, 128), F32)
        gn = jnp.zeros((8, 128), F32)
        for g in range(16):
            ht[:, g * T:(g + 1) * T] = h_ref[g].T
            dl[:, g * T:(g + 1) * T] = g_ref[g, :E, :].astype(BF16)
            gbr = gbr + g_ref[g, :E, :]
            gn = gn + g_ref[g, E:, :]
        gbr_ref[...] = jnp.sum(gbr, axis=1, keepdims=True)
        gn_ref[...] = gn
        gr_ref[...] = jnp.dot(dl[...], h_ref[...].reshape(16 * T, D), preferred_element_type=F32).T

    @pl.when(pl.program_id(1) == 0)
    def _():
        for g in range(16):
            at[:, g * T:(g + 1) * T] = a_ref[0, g * T:(g + 1) * T, :].T

    ggu_ref[0] = jnp.dot(ht[...], c_ref[0], preferred_element_type=F32)
    gdn_ref[0] = jnp.dot(at[...], v_ref[0], preferred_element_type=F32)


def block_body(x_tokens, expert_idx, d_out, norm_w, w_router, b_router, w_gate_up, b_gate_up, w_down, b_down):
    vm = pl.BlockSpec(memory_space=pltpu.VMEM)
    hb = pl.BlockSpec(memory_space=pl.ANY)
    s = jax.ShapeDtypeStruct
    n = 16 * T
    out = pl.pallas_call(
        block_kernel,
        out_shape=(s((T, D), BF16), s((T, D), BF16), s((EL, 1, D), F32), s((EL, 1, D), F32), s((16, 40, 128), F32),
                   s((16, T, D), BF16), s((EL, n, F), BF16), s((EL, n, 2 * F), BF16), s((EL, n, D), BF16)),
        in_specs=[vm, vm, vm, vm, vm, vm, hb, vm, hb, vm],
        out_specs=(vm, vm, vm, vm, vm, hb, hb, hb, hb),
        scratch_shapes=[
            pltpu.VMEM((16, T, 2 * D), BF16),
            pltpu.VMEM((16, E, T), F32),
            pltpu.VMEM((T, E), F32),
            pltpu.VMEM((EL, 2 * T, 128), F32),
            pltpu.VMEM((EL, D, 2 * F), BF16),
            pltpu.VMEM((EL, F, D), BF16),
            pltpu.VMEM((2 * T, 2 * F), F32),
            pltpu.VMEM((2 * T, F), F32),
            pltpu.VMEM((2, 2 * T, F), BF16),
            pltpu.VMEM((2, 2 * T, 2 * F), BF16),
            pltpu.VMEM((2, 2 * T, D), BF16),
            pltpu.VMEM((2 * T, D), F32),
            pltpu.VMEM((4, 2, T, WR), F32),
            pltpu.VMEM((4, T, WR), F32),
            pltpu.VMEM((3, T, WR), F32),
            pltpu.VMEM((16, 40, 128), F32),
            pltpu.VMEM((EL, 8, 2 * F), F32),
            pltpu.VMEM((EL, 8, D), F32),
            pltpu.SemaphoreType.DMA((15,)),
            pltpu.SemaphoreType.DMA((15,)),
            pltpu.SemaphoreType.DMA((15,)),
            pltpu.SemaphoreType.DMA((15,)),
            pltpu.SemaphoreType.DMA((4,)),
            pltpu.SemaphoreType.DMA((4,)),
            pltpu.SemaphoreType.DMA((3,)),
            pltpu.SemaphoreType.DMA((3,)),
            pltpu.SemaphoreType.DMA((16,)),
            pltpu.SemaphoreType.DMA((16,)),
            pltpu.SemaphoreType.DMA((2, EL)),
            pltpu.SemaphoreType.DMA((3, 2)),
            pltpu.SemaphoreType.DMA,
        ],
        compiler_params=pltpu.CompilerParams(collective_id=0, has_side_effects=True, vmem_limit_bytes=60 * 1024 * 1024),
        name="moe_block",
    )(x_tokens, expert_idx, d_out, norm_w.reshape(1, D), w_router, b_router.reshape(1, E),
      w_gate_up, b_gate_up.reshape(EL, 1, 2 * F), w_down, b_down.reshape(EL, 1, D))
    y_out, d_tok, gb_gu, gb_dn, gath, h_all, a_all, c_all, v_all = out
    half = D // 2
    g_gu, g_dn, g_r, g_br, g_n = pl.pallas_call(
        grads_kernel,
        grid=(EL, 2),
        out_shape=(s((EL, D, 2 * F), F32), s((EL, F, D), F32), s((D, E), F32), s((E, 1), F32), s((8, 128), F32)),
        in_specs=[
            pl.BlockSpec((16, T, D), lambda j, t: (0, 0, 0)),
            pl.BlockSpec((1, n, F), lambda j, t: (j, 0, 0)),
            pl.BlockSpec((1, n, half), lambda j, t: (j, 0, t)),
            pl.BlockSpec((1, n, half), lambda j, t: (j, 0, t)),
            pl.BlockSpec((16, 40, 128), lambda j, t: (0, 0, 0)),
        ],
        out_specs=(
            pl.BlockSpec((1, D, half), lambda j, t: (j, 0, t)),
            pl.BlockSpec((1, F, half), lambda j, t: (j, 0, t)),
            pl.BlockSpec((D, E), lambda j, t: (0, 0)),
            pl.BlockSpec((E, 1), lambda j, t: (0, 0)),
            pl.BlockSpec((8, 128), lambda j, t: (0, 0)),
        ),
        scratch_shapes=[pltpu.VMEM((D, n), BF16), pltpu.VMEM((F, n), BF16), pltpu.VMEM((E, n), BF16)],
        compiler_params=pltpu.CompilerParams(dimension_semantics=("arbitrary", "arbitrary"), vmem_limit_bytes=60 * 1024 * 1024),
        name="weight_grads",
    )(h_all, a_all, c_all, v_all, gath)
    return (y_out, d_tok, g_gu, gb_gu.reshape(EL, 2 * F), g_dn, gb_dn.reshape(EL, D), g_r, g_br.reshape(E), g_n.reshape(D))


def solution(mesh):
    tok = P(("dp", "ep"), None)
    w3 = P("ep", None, None)
    w2 = P("ep", None)
    in_specs = (tok, tok, tok, P(), P(), P(), w3, w2, w3, w2)
    out_specs = (tok, tok, w3, w2, w3, w2, P(), P(), P())
    return jax.shard_map(block_body, mesh=mesh, in_specs=in_specs, out_specs=out_specs, check_vma=False)
```

time: 1490 us -> 164 us (0.11)
  other arithmetic: 558 us -> 1.34 us
  waiting for transfers between devices: 467 us -> 0 us
  local copies, waits for them, and re-layouts: 293 us -> 11.7 us
  Pallas kernels: 81.1 us -> 149 us
  blocking collectives: 64.7 us -> 0 us
    psum x2 -> x0, waiting for transfers between devices: 454 us -> none  [the longest x1 454 us: block_body(): grad_gate_up = lax.psum(grad_gate_up, 'dp')]
    scatter-add x6 -> x0, other arithmetic: 404 us -> none  [the longest x1 75.9 us: block_body(): jax.ops.segment_sum(pair_prob[:, None] * y_pair, tok_of, num_segments=n_all)]
    gather x11 -> x0, local copies, waits for them, and re-layouts: 254 us -> none  [the longest x1 45.5 us: block_body(): pair_prob = jnp.where(valid_pair, prob_all.reshape(-1)[pair_order], 0.0)]
    pallas_call x0 -> x2, Pallas kernels: none -> 149 us  [the longest x1 111 us: block_body(): pl.pallas_call(block_kernel, out_shape=(s((T, D), BF16), s((T, D), BF16),...]
    select_n x6 -> x0, other arithmetic: 62.4 us -> none  [the longest x1 33.4 us: block_body(): jnp.where(valid_col, lax.ragged_dot(h_rows, w_gate_up, group_sizes, prefe...]
    another operation x4 -> x0, Pallas kernels: 54 us -> none
    convert_element_type x6 -> x0, other arithmetic: 53.7 us -> none  [the longest x1 19.3 us: block_body(): d_gu_bf = d_gu.astype(jnp.bfloat16)]
    psum x2 -> x0, blocking collectives: 44.8 us -> none  [the longest x1 35.2 us: block_body(): grad_b_router = lax.psum(grad_b_router, ('dp', 'ep'))]
  transfers between devices with their start and end apart: 7 -> 0, of which waited for: 2 -> 0; matrix products, arithmetic and copies ran while one was open for 35% -> 0% of each run, Pallas kernels for 4% -> 0%
where the time goes in v1:
time: 164 us; the launch traced here: 163 us
  Pallas kernels  149 us (91%)
  local copies, waits for them, and re-layouts  11.7 us (7%)
    pallas_call x1, Pallas kernels, block_body(): pl.pallas_call(block_kernel, out_shape=(s((T, D), BF16), s((T, D), BF16),...  111 us
    pallas_call x1, Pallas kernels, block_body(): pl.pallas_call(grads_kernel, grid=(EL, 2), out_shape=(s((EL, D, 2 * F), F...  37.8 us
    unnamed x10, local copies, waits for them, and re-layouts  7.73 us

profile of v1, /device:TPU:0, one launch (start us, length us, event | category | flops | bytes accessed | tf_op | source)
XLA Modules:
  0.0 162.9 jit_solution(9128987227190536077)
XLA Ops:
  0.6 1.3 reshape.42.nw_ref
  1.9 1.3 reshape.44.bgu_ref
  3.3 1.3 reshape.45.bdn_ref
  4.6 1.4 copy.22.idx_ref
  6.0 1.7 %copy.23.wr_ref = bf16[1024,32]{1,0:T(8,128)(2,1)} copy(bf16[1024,32]{0,1:T(8,128)(2,1)} %param.14) | data formatting | bytes 131072 | tf_op args[4]
  7.7 111.4 %moe_block.1 = (bf16[128,1024]{1,0:T(8,128)(2,1)}, bf16[128,1024]{1,0:T(8,128)(2,1)}, f32[4,1,1024]{2,1,0:T(1,128)}, f32[4,1,1024]{2,1,0:T(1,128)}, f32[16,40,12...) custom-call(bf16[128,1024]{1,0:T(8,128)(2,1)} %x_ref.1, ...), custom_call_target="tpu_custom_call" | custom-call | tf_op jit(solution)/shard_map/moe_block/pallas_call | solution.py:339
  119.1 1.4 copy_bitcast_fusion
  120.5 0.0 copy-start.1
  120.5 0.0 copy-start
  120.5 37.8 %weight_grads.1 = (f32[4,1024,1024]{2,1,0:T(8,128)}, f32[4,512,1024]{2,1,0:T(8,128)}, f32[1024,32]{1,0:T(8,128)}, f32[32,1]{1,0:T(8,128)}, f32[8,128]{1,0:T(8,128)}) custom-call(bf16[16,128,1024]{2,1,0:T(8,128)(2,1)} %get-tuple-element.25.h_ref, bf16[4,2048,512]{2,1,0:T(8,128)(2,1)} %get-tuple-element.26.a_ref, ...), custom_call_target="tpu_custom_call" | custom-call | tf_op jit(solution)/shard_map/weight_grads/pallas_call | solution.py:384
  158.2 1.3 reduce
  159.6 1.9 %copy.24 = f32[1024,32]{0,1:T(8,128)} copy(f32[1024,32]{1,0:T(8,128)} %get-tuple-element.52) | data formatting | bytes 262144
  161.5 0.0 copy-done.1
  161.5 0.7 copy.31
  162.2 0.0 copy-done
  162.2 0.7 copy.32
Async XLA Ops:
  120.5 41.0 %copy-start.1 = (bf16[128,1024]{1,0:T(8,128)(2,1)S(1)}, bf16[128,1024]{1,0:T(8,128)(2,1)}, u32[]{:S(2)}) copy-start(bf16[128,1024]{1,0:T(8,128)(2,1)} %get-tuple-element.66) | copy-start | bytes 786436
  120.5 41.7 %copy-start = (bf16[128,1024]{1,0:T(8,128)(2,1)S(1)}, bf16[128,1024]{1,0:T(8,128)(2,1)}, u32[]{:S(2)}) copy-start(bf16[128,1024]{1,0:T(8,128)(2,1)} %get-tuple-element.67) | copy-start | bytes 786436

commit v2 on v1

v2 whole, which is shorter than its diff:
```python
import functools

import jax
import jax.numpy as jnp
from jax import lax
from jax.experimental import pallas as pl
from jax.experimental.pallas import tpu as pltpu
from jax.sharding import PartitionSpec as P

SWIGLU_LIMIT = 7.0
SIG_ALPHA = 1.702
NORM_EPS = 1e-5
F32 = jnp.float32
BF16 = jnp.bfloat16
MESH = pl.DeviceIdType.MESH
NT = (((1,), (1,)), ((), ()))
D = 1024
F = 512
E = 32
EL = 4
T = 128
WR = 2 * D + 128
CA = 1280
CB = WR - CA
MERGE_IT = 8
ROWS = 16
COLS = 128


def block_kernel(x_ref, idx_ref, dout_ref, nw_ref, wr_ref, br_ref, wgu_hbm, bgu_ref, wdn_hbm, bdn_ref,
                 y_out, dt_out, gbgu_ref, gbdn_ref, g_out, h_hbm, a_hbm, c_hbm, v_hbm,
                 hd, pt, ph, pb, wgu, wdn, gu, da, a_st, c_st, v_st, dyf, qs, bg, bd, part, rd, rxa, rxb, rya, ryb, ria, rib, gath, accg, accd,
                 ag_s, ag_r, pt_s, pt_r, d2d_s, d2d_r, rs_s, rs_r, g_s, g_r, w_sem, st_sem, h_sem):
    d = lax.axis_index("dp")
    e = lax.axis_index("ep")
    k = e % 2
    cx = (e // 2) % 2
    cy = e // 4

    def chip(m):
        return ((cy + m // 2) % 2) * 2 + (cx + m % 2) % 2

    def ep_of(m, kk):
        return chip(m) * 2 + kk

    def dev(r):
        kk = (k + r % 2) % 2
        xx = (cx + (r // 2) % 2) % 2
        yy = (cy + (r // 4) % 2) % 2
        return ((d + r // 8) % 2, (yy * 2 + xx) * 2 + kk)

    sib = (d, e + 1 - 2 * k)
    zp = (1 - d, e)
    me = d * 8 + e

    for j in range(EL):
        pltpu.make_async_copy(wgu_hbm.at[j], wgu.at[j], w_sem.at[0, j]).start()
        pltpu.make_async_copy(wdn_hbm.at[j], wdn.at[j], w_sem.at[1, j]).start()

    barrier = pltpu.get_barrier_semaphore()

    @pl.loop(1, 16)
    def _(r):
        pl.semaphore_signal(barrier, inc=1, device_id=dev(r), device_id_type=MESH)

    x = x_ref[...].astype(F32)
    inv = lax.rsqrt(jnp.mean(x * x, axis=-1, keepdims=True) + NORM_EPS)
    normed = x * inv
    h = (normed * nw_ref[...].astype(F32).reshape(1, D)).astype(BF16)
    hd[me, :, :D] = h
    hd[me, :, D:] = dout_ref[...]
    logits = lax.dot_general(h, wr_ref[...], NT, preferred_element_type=F32) + br_ref[...].reshape(1, E)
    idx = idx_ref[...].T
    lane = lax.broadcasted_iota(jnp.int32, (T, E), 1)
    hit = idx[:, 0:1] == lane
    for i in range(1, 8):
        hit = hit | (idx[:, i:i + 1] == lane)
    top = jnp.max(jnp.where(hit, logits, -jnp.inf), axis=-1, keepdims=True)
    ex = jnp.where(hit, jnp.exp(logits - top), 0.0)
    prob = ex / jnp.sum(ex, axis=-1, keepdims=True)
    ph[...] = prob
    pt[me] = prob.T

    pl.semaphore_wait(barrier, 15)

    def ag(i, g, to):
        return (pltpu.make_async_remote_copy(hd.at[g], hd.at[g], ag_s.at[i], ag_r.at[i], device_id=to, device_id_type=MESH),
                pltpu.make_async_remote_copy(pt.at[g], pt.at[g], pt_s.at[i], pt_r.at[i], device_id=to, device_id_type=MESH))

    def ag_send(i, g, to):
        for cp in ag(i, g, to):
            cp.start()

    def ag_wait(i, g):
        for cp in ag(i, g, sib):
            cp.wait_recv()

    ag_send(7, me, sib)
    ag_send(0, me, (d, ep_of(1, k)))
    ag_send(1, me, (d, ep_of(2, k)))
    ag_send(3, me, zp)
    ag_send(2, me, (d, ep_of(3, k)))

    for j in range(EL):
        bg[j] = bgu_ref[j:j + 1, :]
        bd[j] = bdn_ref[j:j + 1, :]
    accg[...] = jnp.zeros_like(accg)
    accd[...] = jnp.zeros_like(accd)

    def rd_copy(m):
        return pltpu.make_async_remote_copy(part.at[m, 1 - k], rd.at[m], d2d_s.at[m], d2d_r.at[m], device_id=sib, device_id_type=MESH)

    def rs_copy(i):
        m, first, dst, to = ((1, True, rxa, 1), (3, True, ria, 1), (1, False, rxb, 1),
                             (2, False, ryb, 2), (3, False, rib, 2), (2, True, rya, 2))[i]
        cols = pl.ds(0, CA) if first else pl.ds(CA, CB)
        return pltpu.make_async_remote_copy(part.at[m, k, :, cols], dst, rs_s.at[i], rs_r.at[i],
                                            device_id=(d, ep_of(to, k)), device_id_type=MESH)

    def merge(m, cols, src):
        part[m, k, :, cols] += src[...]

    def st_copies(par, j, slot):
        return (pltpu.make_async_copy(a_st.at[par], a_hbm.at[j, pl.ds(slot * T, 2 * T)], st_sem.at[0, par]),
                pltpu.make_async_copy(c_st.at[par], c_hbm.at[j, pl.ds(slot * T, 2 * T)], st_sem.at[1, par]),
                pltpu.make_async_copy(v_st.at[par], v_hbm.at[j, pl.ds(slot * T, 2 * T)], st_sem.at[2, par]))

    def h_copy(slot):
        return pltpu.make_async_copy(hd.at[pl.ds(slot, 2), :, pl.ds(0, D)], h_hbm.at[pl.ds(slot, 2)], h_sem)

    def stage_probs(slot):
        sub = lax.broadcasted_iota(jnp.int32, (E, T), 0)
        for cc in range(2):
            dyf[cc * T:(cc + 1) * T, :] = hd[slot + cc, :, D:].astype(F32)
            rows = pt[slot + cc]
            for j in range(EL):
                row = jnp.sum(jnp.where(sub == 4 * e + j, rows, 0.0), axis=0, keepdims=True)
                pb[j, cc * T:(cc + 1) * T, :] = jnp.broadcast_to(row, (T, T)).T

    def expert(m, j, slot, own):
        par = j % 2
        hx = hd[pl.ds(slot, 2), :, :D].reshape(2 * T, D)
        gu[...] = jnp.dot(hx, wgu[j], preferred_element_type=F32)
        for c in range(0, D, 128):
            acc = jnp.zeros((8, 128), F32)
            for r in range(0, 2 * T, ROWS):
                v = pb[j, r:r + ROWS, :] * dyf[r:r + ROWS, c:c + 128]
                v_st[par, r:r + ROWS, c:c + 128] = v.astype(BF16)
                acc = acc + jnp.sum(v.reshape(ROWS // 8, 8, 128), axis=0)
            accd[j, :, c:c + 128] += acc
        da[...] = lax.dot_general(v_st[par], wdn[j], NT, preferred_element_type=F32)
        for c in range(0, F, COLS):
            accl = jnp.zeros((8, COLS), F32)
            accu = jnp.zeros((8, COLS), F32)
            for r in range(0, 2 * T, ROWS):
                gpre = gu[r:r + ROWS, c:c + COLS] + bg[j, :, c:c + COLS]
                upre = gu[r:r + ROWS, F + c:F + c + COLS] + bg[j, :, F + c:F + c + COLS]
                gc = jnp.minimum(gpre, SWIGLU_LIMIT)
                uc = jnp.clip(upre, -SWIGLU_LIMIT, SWIGLU_LIMIT)
                sg = jax.nn.sigmoid(SIG_ALPHA * gc)
                gs = gc * sg
                u1 = uc + 1.0
                a_st[par, r:r + ROWS, c:c + COLS] = (gs * u1).astype(BF16)
                dact = da[r:r + ROWS, c:c + COLS]
                dg = jnp.where(gpre < SWIGLU_LIMIT, dact * u1 * sg * (1.0 + SIG_ALPHA * gc * (1.0 - sg)), 0.0)
                du = jnp.where(jnp.abs(upre) < SWIGLU_LIMIT, dact * gs, 0.0)
                c_st[par, r:r + ROWS, c:c + COLS] = dg.astype(BF16)
                c_st[par, r:r + ROWS, F + c:F + c + COLS] = du.astype(BF16)
                accl = accl + jnp.sum(dg.reshape(ROWS // 8, 8, COLS), axis=0)
                accu = accu + jnp.sum(du.reshape(ROWS // 8, 8, COLS), axis=0)
            accg[j, :, c:c + COLS] += accl
            accg[j, :, F + c:F + c + COLS] += accu
        if own:
            for c in range(0, D, 256):
                yv = jnp.dot(a_st[par], wdn[j, :, c:c + 256], preferred_element_type=F32)
                for r in range(0, 2 * T, ROWS):
                    p = pb[j, r:r + ROWS, :]
                    cc, rt = r // T, r % T
                    q = None
                    for b in range(0, 256, 128):
                        y1 = yv[r:r + ROWS, b:b + 128] + bd[j, :, c + b:c + b + 128]
                        part[m, cc, rt:rt + ROWS, c + b:c + b + 128] += p * y1
                        t = dyf[r:r + ROWS, c + b:c + b + 128] * y1
                        q = t if q is None else q + t
                    if c == 0:
                        qs[r:r + ROWS, :] = q
                    else:
                        qs[r:r + ROWS, :] += q
            for c in range(0, D, 256):
                dv = lax.dot_general(c_st[par], wgu[j, c:c + 256, :], NT, preferred_element_type=F32)
                part[m, :, :, D + c:D + c + 256] += dv.reshape(2, T, 256)
            lanes = lax.broadcasted_iota(jnp.int32, (T, 128), 1)
            for cc in range(2):
                q = jnp.sum(qs[cc * T:(cc + 1) * T, :], axis=1, keepdims=True)
                part[m, cc, :, 2 * D:] += jnp.where(lanes == 4 * e + j, q, 0.0)

    def pre_expert(s, j, first):
        par = j % 2

        @pl.when(s * EL + j >= first)
        def _():
            for cp in st_copies(par, j, 0):
                cp.wait()

    @pl.loop(0, 4)
    def _(s):
        m = s + (s // 2) * (1 - 2 * (s % 2))
        slot = d * 8 + chip(m) * 2
        ag_wait(7 + m, 0)
        h_copy(slot).start()
        stage_probs(slot)
        part[m] = jnp.zeros((2, T, WR), F32)

        @pl.loop(0, EL)
        def _(j):
            @pl.when(s == 0)
            def _():
                pltpu.make_async_copy(wgu_hbm.at[j], wgu.at[j], w_sem.at[0, j]).wait()
                pltpu.make_async_copy(wdn_hbm.at[j], wdn.at[j], w_sem.at[1, j]).wait()

            pre_expert(s, j, 2)
            expert(m, j, slot, True)
            it = s * EL + j

            @pl.when(it == 4)
            def _():
                rd_copy(0).wait_recv()
                merge(0, slice(None), rd.at[0])

            @pl.when(it == 8)
            def _():
                rd_copy(1).wait_recv()
                merge(1, slice(None), rd.at[1])

            @pl.when(it == 12)
            def _():
                rd_copy(3).wait_recv()
                merge(3, slice(None), rd.at[3])

            @pl.when(it == 15)
            def _():
                rs_copy(4).wait_recv()
                merge(1, slice(CA, WR), rib)

            for cp in st_copies(j % 2, j, slot):
                cp.start()

            def fetch(mm):
                ag_wait(mm - 1, 0)
                g = d * 8 + ep_of(mm, k)
                ag_send(7 + mm, g, sib)
                ag_send(3 + mm, g, zp)

            @pl.when(it == 3)
            def _():
                fetch(1)

            @pl.when(it == 5)
            def _():
                fetch(2)

            @pl.when(it == 6)
            def _():
                ag_wait(3, 0)
                ag_send(11, (1 - d) * 8 + e, sib)

            @pl.when(it == 7)
            def _():
                fetch(3)

            @pl.when(it == 8)
            def _():
                rs_copy(0).start()

            @pl.when(it == 12)
            def _():
                rs_copy(1).start()
                rs_copy(4).start()

            @pl.when(it == 15)
            def _():
                rs_copy(2).start()

            @pl.when(j == EL - 1)
            def _():
                rd_copy(m).start()

        h_copy(slot).wait()

    @pl.loop(0, 4)
    def _(m):
        slot = (1 - d) * 8 + chip(m) * 2
        ag_wait(11 + m, 0)
        h_copy(slot).start()
        stage_probs(slot)

        @pl.loop(0, EL)
        def _(j):
            pre_expert(m, j, 0)
            expert(m, j, slot, False)
            it = m * EL + j

            @pl.when(it == 1)
            def _():
                rd_copy(2).wait_recv()
                merge(2, slice(None), rd.at[2])

            @pl.when(it == MERGE_IT)
            def _():
                rs_copy(1).wait_recv()
                merge(2, slice(0, CA), ria)

            for cp in st_copies(j % 2, j, slot):
                cp.start()

            @pl.when((j == 2) & (m < 3))
            def _():
                ag_wait(4 + m, 0)
                ag_send(12 + m, (1 - d) * 8 + ep_of(m + 1, k), sib)

            @pl.when(it == 1)
            def _():
                rs_copy(3).start()

            @pl.when(it == MERGE_IT)
            def _():
                rs_copy(5).start()

        h_copy(slot).wait()

    for par in range(2):
        for cp in st_copies(par, 0, 0):
            cp.wait()
    for j in range(EL):
        gbgu_ref[j:j + 1, :] = jnp.sum(accg[j], axis=0, keepdims=True)
        gbdn_ref[j:j + 1, :] = jnp.sum(accd[j], axis=0, keepdims=True)

    for i in (0, 2, 3, 5):
        rs_copy(i).wait_recv()
    x = x_ref[...].astype(F32)
    inv = lax.rsqrt(jnp.mean(x * x, axis=-1, keepdims=True) + NORM_EPS)
    normed = x * inv
    tot_a = part[0, k, :, :CA] + rxa[...] + rya[...]
    tot_b = part[0, k, :, CA:] + rxb[...] + ryb[...]
    y_out[...] = (x + tot_a[:, :D]).astype(BF16)
    prob = ph[...]
    q = tot_b[:, 2 * D - CA:2 * D - CA + E]
    dlog = prob * (q - jnp.sum(prob * q, axis=1, keepdims=True))
    d_h = jnp.concatenate([tot_a[:, D:], tot_b[:, :2 * D - CA]], axis=1) + jnp.dot(dlog.astype(BF16), wr_ref[...], preferred_element_type=F32)
    gath[me, :E, :] = dlog.T
    gn = jnp.sum(d_h * normed, axis=0, keepdims=True)
    for i in range(8):
        gath[me, E + i:E + i + 1, :] = gn[:, i * 128:(i + 1) * 128]
    dn = d_h * nw_ref[...].astype(F32).reshape(1, D)
    dt_out[...] = (dout_ref[...].astype(F32) + inv * (dn - normed * jnp.mean(dn * normed, axis=-1, keepdims=True))).astype(BF16)

    def g_copy(r):
        return pltpu.make_async_remote_copy(gath.at[me], gath.at[me], g_s.at[r], g_r.at[r], device_id=dev(r), device_id_type=MESH)

    @pl.loop(1, 16)
    def _(r):
        g_copy(r).start()

    for i in range(15):
        for cp in ag(i, 0, sib):
            cp.wait_send()
    for m in range(4):
        rd_copy(m).wait_send()
    for i in range(6):
        rs_copy(i).wait_send()

    @pl.loop(1, 16)
    def _(r):
        g_copy(r).wait()

    g_out[...] = gath[...]


def grads_kernel(h_ref, a_ref, c_ref, v_ref, g_ref, yi_ref, ti_ref, bgi_ref, bdi_ref,
                 ggu_ref, gdn_ref, gr_ref, gbr_ref, gn_ref, yo_ref, to_ref, bgo_ref, bdo_ref, ht, at, dl):
    first = (pl.program_id(0) == 0) & (pl.program_id(1) == 0)

    @pl.when(first)
    def _():
        gbr = jnp.zeros((E, 128), F32)
        gn = jnp.zeros((8, 128), F32)
        for g in range(16):
            ht[:, g * T:(g + 1) * T] = h_ref[g].T
            dl[:, g * T:(g + 1) * T] = g_ref[g, :E, :].astype(BF16)
            gbr = gbr + g_ref[g, :E, :]
            gn = gn + g_ref[g, E:, :]
        gbr_ref[...] = jnp.sum(gbr.T, axis=0, keepdims=True)
        gn_ref[...] = gn
        yo_ref[...] = yi_ref[...]
        to_ref[...] = ti_ref[...]
        bgo_ref[...] = bgi_ref[...]
        bdo_ref[...] = bdi_ref[...]
        gr_ref[...] = jnp.dot(dl[...], h_ref[...].reshape(16 * T, D), preferred_element_type=F32)

    for g in range(16):
        at[:, g * T:(g + 1) * T] = a_ref[0, g * T:(g + 1) * T, :].T
    ggu_ref[0] = jnp.dot(ht[...], c_ref[0], preferred_element_type=F32)
    gdn_ref[0] = jnp.dot(at[...], v_ref[0], preferred_element_type=F32)


def block_body(x_tokens, expert_idx, d_out, norm_w, w_router, b_router, w_gate_up, b_gate_up, w_down, b_down):
    vm = pl.BlockSpec(memory_space=pltpu.VMEM)
    hb = pl.BlockSpec(memory_space=pl.ANY)
    s = jax.ShapeDtypeStruct
    n = 16 * T
    out = pl.pallas_call(
        block_kernel,
        out_shape=(s((T, D), BF16), s((T, D), BF16), s((EL, D), F32), s((EL, D), F32), s((16, 40, 128), F32),
                   s((16, T, D), BF16), s((EL, n, F), BF16), s((EL, n, 2 * F), BF16), s((EL, n, D), BF16)),
        in_specs=[vm, vm, vm, vm, vm, vm, hb, vm, hb, vm],
        out_specs=(vm, vm, vm, vm, vm, hb, hb, hb, hb),
        scratch_shapes=[
            pltpu.VMEM((16, T, 2 * D), BF16),
            pltpu.VMEM((16, E, T), F32),
            pltpu.VMEM((T, E), F32),
            pltpu.VMEM((EL, 2 * T, 128), F32),
            pltpu.VMEM((EL, D, 2 * F), BF16),
            pltpu.VMEM((EL, F, D), BF16),
            pltpu.VMEM((2 * T, 2 * F), F32),
            pltpu.VMEM((2 * T, F), F32),
            pltpu.VMEM((2, 2 * T, F), BF16),
            pltpu.VMEM((2, 2 * T, 2 * F), BF16),
            pltpu.VMEM((2, 2 * T, D), BF16),
            pltpu.VMEM((2 * T, D), F32),
            pltpu.VMEM((2 * T, 128), F32),
            pltpu.VMEM((EL, 1, 2 * F), F32),
            pltpu.VMEM((EL, 1, D), F32),
            pltpu.VMEM((4, 2, T, WR), F32),
            pltpu.VMEM((4, T, WR), F32),
            pltpu.VMEM((T, CA), F32),
            pltpu.VMEM((T, CB), F32),
            pltpu.VMEM((T, CA), F32),
            pltpu.VMEM((T, CB), F32),
            pltpu.VMEM((T, CA), F32),
            pltpu.VMEM((T, CB), F32),
            pltpu.VMEM((16, 40, 128), F32),
            pltpu.VMEM((EL, 8, 2 * F), F32),
            pltpu.VMEM((EL, 8, D), F32),
            pltpu.SemaphoreType.DMA((15,)),
            pltpu.SemaphoreType.DMA((15,)),
            pltpu.SemaphoreType.DMA((15,)),
            pltpu.SemaphoreType.DMA((15,)),
            pltpu.SemaphoreType.DMA((4,)),
            pltpu.SemaphoreType.DMA((4,)),
            pltpu.SemaphoreType.DMA((6,)),
            pltpu.SemaphoreType.DMA((6,)),
            pltpu.SemaphoreType.DMA((16,)),
            pltpu.SemaphoreType.DMA((16,)),
            pltpu.SemaphoreType.DMA((2, EL)),
            pltpu.SemaphoreType.DMA((3, 2)),
            pltpu.SemaphoreType.DMA,
        ],
        compiler_params=pltpu.CompilerParams(collective_id=0, has_side_effects=True, vmem_limit_bytes=60 * 1024 * 1024),
        name="moe_block",
    )(x_tokens, expert_idx.T, d_out, norm_w, w_router.T, b_router, w_gate_up, b_gate_up, w_down, b_down)
    y_out, d_tok, gb_gu, gb_dn, gath, h_all, a_all, c_all, v_all = out
    half = D // 2

    def full(shape):
        return pl.BlockSpec(shape, lambda j, t: (0, 0))

    g_gu, g_dn, g_r, g_br, g_n, y_out, d_tok, gb_gu, gb_dn = pl.pallas_call(
        grads_kernel,
        grid=(EL, 2),
        out_shape=(s((EL, D, 2 * F), F32), s((EL, F, D), F32), s((E, D), F32), s((1, E), F32), s((8, 128), F32),
                   s((T, D), BF16), s((T, D), BF16), s((EL, D), F32), s((EL, D), F32)),
        in_specs=[
            pl.BlockSpec((16, T, D), lambda j, t: (0, 0, 0)),
            pl.BlockSpec((1, n, F), lambda j, t: (j, 0, 0)),
            pl.BlockSpec((1, n, half), lambda j, t: (j, 0, t)),
            pl.BlockSpec((1, n, half), lambda j, t: (j, 0, t)),
            pl.BlockSpec((16, 40, 128), lambda j, t: (0, 0, 0)),
            full((T, D)), full((T, D)), full((EL, D)), full((EL, D)),
        ],
        out_specs=(
            pl.BlockSpec((1, D, half), lambda j, t: (j, 0, t)),
            pl.BlockSpec((1, F, half), lambda j, t: (j, 0, t)),
            pl.BlockSpec((E, D), lambda j, t: (0, 0)),
            pl.BlockSpec((1, E), lambda j, t: (0, 0)),
            pl.BlockSpec((8, 128), lambda j, t: (0, 0)),
            full((T, D)), full((T, D)), full((EL, D)), full((EL, D)),
        ),
        scratch_shapes=[pltpu.VMEM((D, n), BF16), pltpu.VMEM((F, n), BF16), pltpu.VMEM((E, n), BF16)],
        compiler_params=pltpu.CompilerParams(dimension_semantics=("arbitrary", "arbitrary"), vmem_limit_bytes=60 * 1024 * 1024),
        name="weight_grads",
    )(h_all, a_all, c_all, v_all, gath, y_out, d_tok, gb_gu, gb_dn)
    return (y_out, d_tok, g_gu, gb_gu, g_dn, gb_dn, g_r.T, g_br.reshape(E), g_n.reshape(D))


def solution(mesh):
    tok = P(("dp", "ep"), None)
    w3 = P("ep", None, None)
    w2 = P("ep", None)
    in_specs = (tok, tok, tok, P(), P(), P(), w3, w2, w3, w2)
    out_specs = (tok, tok, w3, w2, w3, w2, P(), P(), P())
    return jax.shard_map(block_body, mesh=mesh, in_specs=in_specs, out_specs=out_specs, check_vma=False)
```

time: 164 us -> 139 us (0.85)
  local copies, waits for them, and re-layouts: 11.7 us -> 0 us
  Pallas kernels: 149 us -> 138 us
    pallas_call x1, Pallas kernels: 111 us -> 102 us  [block_body(): pl.pallas_call(block_kernel, out_shape=(s((T, D), BF16), s((T, D), BF16),...]
    unnamed x10 -> x0, local copies, waits for them, and re-layouts: 7.73 us -> none
    reshape x3 -> x0, local copies, waits for them, and re-layouts: 3.94 us -> none  [the longest x1 1.33 us: block_body(): b_gate_up.reshape(EL, 1, 2 * F)]
    pallas_call x1, Pallas kernels: 37.8 us -> 36.1 us  [block_body(): pl.pallas_call(grads_kernel, grid=(EL, 2), out_shape=(s((EL, D, 2 * F), F...]
where the time goes in v2:
time: 139 us
  Pallas kernels  138 us (99%)
    pallas_call x1, Pallas kernels, block_body(): pl.pallas_call(block_kernel, out_shape=(s((T, D), BF16), s((T, D), BF16),...  102 us
    pallas_call x1, Pallas kernels, block_body(): pl.pallas_call(grads_kernel, grid=(EL, 2), out_shape=(s((EL, D, 2 * F), F...  36.1 us

profile of v2, /device:TPU:0, one launch (start us, length us, event | category | flops | bytes accessed | tf_op | source)
XLA Modules:
  0.0 138.5 jit_solution(12055453929751095309)
XLA Ops:
  0.6 101.8 %moe_block.1 = (bf16[128,1024]{1,0:T(8,128)(2,1)}, bf16[128,1024]{1,0:T(8,128)(2,1)}, f32[4,1024]{1,0:T(4,128)}, f32[4,1024]{1,0:T(4,128)}, f32[16,40,128]{2,1,0...) custom-call(bf16[128,1024]{1,0:T(8,128)(2,1)} %x_ref.1, ...), custom_call_target="tpu_custom_call" | custom-call | tf_op jit(solution)/shard_map/moe_block/pallas_call | solution.py:411
  102.5 36.1 %weight_grads.1 = (f32[4,1024,1024]{2,1,0:T(8,128)}, f32[4,512,1024]{2,1,0:T(8,128)}, f32[32,1024]{1,0:T(8,128)}, f32[1,32]{1,0:T(1,128)}, f32[8,128]{1,0:T(8,12...) custom-call(bf16[16,128,1024]{2,1,0:T(8,128)(2,1)} %get-tuple-element.27.h_re, ...), custom_call_target="tpu_custom_call" | custom-call | tf_op jit(solution)/shard_map/weight_grads/pallas_call | solution.py:467

commit v3 on v2

v3 whole, which is shorter than its diff:
```python
import functools

import jax
import jax.numpy as jnp
from jax import lax
from jax.experimental import pallas as pl
from jax.experimental.pallas import tpu as pltpu
from jax.sharding import PartitionSpec as P

SWIGLU_LIMIT = 7.0
SIG_ALPHA = 1.702
NORM_EPS = 1e-5
F32 = jnp.float32
BF16 = jnp.bfloat16
MESH = pl.DeviceIdType.MESH
NT = (((1,), (1,)), ((), ()))
D = 1024
F = 512
E = 32
EL = 4
T = 128
NC = 2
TT = NC * T
FF = NC * F
LN = 128
N = 16 * T
ROWS = 16
COLS = 128
MERGE_IT = 7
FETCH_D = 2


def mid_of(m):
    return (m + 1) // 2 % 2


def col_sum(v):
    return jnp.sum(v, axis=0, keepdims=True)


def row_mean(v):
    return jnp.mean(v, axis=-1, keepdims=True)


def slot_of(m, kk):
    mid = mid_of(m)
    return mid * (1 + m + 4 * kk) + (1 - mid) * (m // 3 * 4 + kk)


def place():
    d = lax.axis_index("dp")
    e = lax.axis_index("ep")
    return d, e, e % 2, (e // 2) % 2, e // 4


def block_kernel(x_ref, idx_ref, dout_ref, nw_ref, wr_ref, br_ref, wgu_hbm, bgu_ref, wdn_hbm, bdn_ref,
                 y_out, dt_out, gbgu_ref, gbdn_ref, gr_out, gn_out, ht_hbm, a_hbm, c_hbm, v_hbm,
                 hd, pt, pb, wgu, wdn, gu, da, a_st, c_st, v_st, dyf, qs, bg, bd, py, pd, rdy, rdd,
                 rxa, rxb, rya, ryb, ria, rib, qt, qbuf, dlog_s, gdl, ggn, ht, accg, accd,
                 ag_s, ag_r, pt_s, pt_r, d2d_s, d2d_r, rs_s, rs_r, q_s, q_r, dl_s, dl_r, gn_s, gn_r, w_sem, st_sem, h_sem):
    d, e, k, cx, cy = place()

    def ep_of(m, kk):
        return (((cy + m // 2) % 2) * 2 + (cx + m % 2) % 2) * 2 + kk

    def dev(r):
        return ((d + r // 8) % 2, ep_of((r // 2) % 4, (k + r % 2) % 2))

    sib = (d, e + 1 - 2 * k)
    zp = (1 - d, e)
    me = d * 8 + e

    for j in range(EL):
        pltpu.make_async_copy(wgu_hbm.at[j], wgu.at[j], w_sem.at[0, j]).start()
        pltpu.make_async_copy(wdn_hbm.at[j], wdn.at[j], w_sem.at[1, j]).start()

    barrier = pltpu.get_barrier_semaphore()

    @pl.loop(1, 16)
    def _(r):
        pl.semaphore_signal(barrier, inc=1, device_id=dev(r), device_id_type=MESH)

    nw = nw_ref[:].astype(F32).reshape(1, D)
    x = x_ref[:].astype(F32)
    inv = lax.rsqrt(row_mean(x * x) + NORM_EPS)
    h = (x * inv * nw).astype(BF16)
    hd[k, :, :D] = h
    hd[k, :, D:] = dout_ref[:]
    logits = lax.dot_general(h, wr_ref[:], NT, preferred_element_type=F32) + br_ref[:].reshape(1, E)
    idx = idx_ref[:].T
    lane = lax.broadcasted_iota(jnp.int32, (T, E), 1)
    hit = idx[:, 0:1] == lane
    for i in range(1, 8):
        hit = hit | (idx[:, i:i + 1] == lane)
    top = jnp.max(jnp.where(hit, logits, -jnp.inf), axis=-1, keepdims=True)
    ex = jnp.where(hit, jnp.exp(logits - top), 0.0)
    pt[k] = (ex / jnp.sum(ex, axis=-1, keepdims=True)).T

    pl.semaphore_wait(barrier, 15)

    def ag_copies(i, src, dst, to):
        return (pltpu.make_async_remote_copy(hd.at[src], hd.at[dst], ag_s.at[i], ag_r.at[i], device_id=to, device_id_type=MESH),
                pltpu.make_async_remote_copy(pt.at[src], pt.at[dst], pt_s.at[i], pt_r.at[i], device_id=to, device_id_type=MESH))

    def ag_send(i, src, dst, to):
        for cp in ag_copies(i, src, dst, to):
            cp.start()

    def ag_wait(i):
        for cp in ag_copies(i, 0, 0, sib):
            cp.wait_recv()

    def near(m):
        ag_send(m - 1, k, slot_of(m, k), (d, ep_of(m, k)))

    def fetch(m):
        ag_wait(m - 1)
        sl = slot_of(m, k)
        ag_send(7 + m, sl, sl, sib)
        ag_send(3 + m, sl, sl + 8, zp)

    def fetch_z(m):
        ag_wait(3 + m)
        sl = slot_of(m, k) + 8
        ag_send(11 + m, sl, sl, sib)

    ag_send(7, k, k, sib)

    @pl.when(k == 0)
    def _():
        near(1)
        near(2)

    ag_send(3, k, k + 8, zp)

    for j in range(EL):
        bg[j] = bgu_ref[j:j + 1, :]
        bd[j] = bdn_ref[j:j + 1, :]
    accg[:] = jnp.zeros_like(accg)
    accd[:] = jnp.zeros_like(accd)

    def mine(m):
        mid = mid_of(m)
        return mid * (1 + 2 * k) + (1 - mid) * (m // 3 * 2), mid * (m - 1) + (1 - mid) * k

    def theirs(m):
        mid = mid_of(m)
        return mid * (3 - 2 * k) + (1 - mid) * (m // 3 * 2), mid * (m - 1) + (1 - mid) * (1 - k)

    def d2d(m, hi):
        s, half = theirs(m)
        src, dst = (pd, rdd) if hi else (py, rdy)
        i = 2 * m + hi
        return pltpu.make_async_remote_copy(src.at[s, half], dst.at[m], d2d_s.at[i], d2d_r.at[i], device_id=sib, device_id_type=MESH)

    def pair_sum(m, hi):
        d2d(m, hi).wait_recv()
        s, half = mine(m)
        buf, src = (pd, rdd) if hi else (py, rdy)
        buf[s, half] += src[m]

    def rs_copy(i):
        m, hi, dst, to = ((1, 0, rxa, 1), (3, 0, ria, 1), (1, 1, rxb, 1),
                          (2, 1, ryb, 2), (3, 1, rib, 2), (2, 0, rya, 2))[i]
        s, half = mine(m)
        return pltpu.make_async_remote_copy((pd if hi else py).at[s, half], dst, rs_s.at[i], rs_r.at[i],
                                            device_id=(d, ep_of(to, k)), device_id_type=MESH)

    def q_copy(m, kk):
        i = m * 2 + (kk + k) % 2
        return pltpu.make_async_remote_copy(qt.at[slot_of(m, kk)], qbuf.at[e], q_s.at[i], q_r.at[i],
                                            device_id=(d, ep_of(m, kk)), device_id_type=MESH)

    def dl_copy(r):
        return pltpu.make_async_remote_copy(gdl.at[me], gdl.at[me], dl_s.at[r], dl_r.at[r], device_id=dev(r), device_id_type=MESH)

    def gn_copy(r):
        return pltpu.make_async_remote_copy(ggn.at[me], ggn.at[me], gn_s.at[r], gn_r.at[r], device_id=dev(r), device_id_type=MESH)

    def st_copies(par, j, slot):
        rows = pl.ds(slot * T, TT)
        return (pltpu.make_async_copy(a_st.at[par], a_hbm.at[j, rows], st_sem.at[0, par]),
                pltpu.make_async_copy(c_st.at[par], c_hbm.at[j, rows], st_sem.at[1, par]),
                pltpu.make_async_copy(v_st.at[par], v_hbm.at[j, rows], st_sem.at[2, par]))

    def ht_copy(i):
        cols = pl.ds(i * EL * T, EL * T)
        return pltpu.make_async_copy(ht.at[:, cols], ht_hbm.at[:, cols], h_sem.at[i])

    def stage_probs(slot):
        sub = lax.broadcasted_iota(jnp.int32, (E, T), 0)
        for cc in range(NC):
            dyf[cc * T:(cc + 1) * T, :] = hd[slot + cc, :, D:].astype(F32)
            rows = pt[slot + cc]
            for j in range(EL):
                row = col_sum(jnp.where(sub == 4 * e + j, rows, 0.0))
                pb[j, cc * T:(cc + 1) * T, :] = jnp.broadcast_to(row, (T, T)).T

    def expert(s, j, slot, own):
        par = j % 2
        hx = hd[pl.ds(slot, 2), :, :D].reshape(TT, D)
        gu[:] = jnp.dot(hx, wgu[j], preferred_element_type=F32)
        for c in range(0, D, LN):
            acc = jnp.zeros((8, LN), F32)
            for r in range(0, TT, ROWS):
                v = pb[j, r:r + ROWS, :] * dyf[r:r + ROWS, c:c + 128]
                v_st[par, r:r + ROWS, c:c + 128] = v.astype(BF16)
                acc = acc + jnp.sum(v.reshape(ROWS // 8, 8, LN), axis=0)
            accd[j, :, c:c + 128] += acc
        da[:] = lax.dot_general(v_st[par], wdn[j], NT, preferred_element_type=F32)
        for c in range(0, F, COLS):
            accl = jnp.zeros((8, COLS), F32)
            accu = jnp.zeros((8, COLS), F32)
            for r in range(0, TT, ROWS):
                gpre = gu[r:r + ROWS, c:c + COLS] + bg[j, :, c:c + COLS]
                upre = gu[r:r + ROWS, F + c:F + c + COLS] + bg[j, :, F + c:F + c + COLS]
                gc = jnp.minimum(gpre, SWIGLU_LIMIT)
                uc = jnp.clip(upre, -SWIGLU_LIMIT, SWIGLU_LIMIT)
                sg = jax.nn.sigmoid(SIG_ALPHA * gc)
                gs = gc * sg
                u1 = uc + 1.0
                a_st[par, r:r + ROWS, c:c + COLS] = (gs * u1).astype(BF16)
                dact = da[r:r + ROWS, c:c + COLS]
                dg = jnp.where(gpre < SWIGLU_LIMIT, dact * u1 * sg * (1.0 + SIG_ALPHA * gc * (1.0 - sg)), 0.0)
                du = jnp.where(jnp.abs(upre) < SWIGLU_LIMIT, dact * gs, 0.0)
                c_st[par, r:r + ROWS, c:c + COLS] = dg.astype(BF16)
                c_st[par, r:r + ROWS, F + c:F + c + COLS] = du.astype(BF16)
                accl = accl + jnp.sum(dg.reshape(ROWS // 8, 8, COLS), axis=0)
                accu = accu + jnp.sum(du.reshape(ROWS // 8, 8, COLS), axis=0)
            accg[j, :, c:c + COLS] += accl
            accg[j, :, F + c:F + c + COLS] += accu
        if own:
            for c in range(0, D, 256):
                yv = jnp.dot(a_st[par], wdn[j, :, c:c + 256], preferred_element_type=F32)
                for r in range(0, TT, ROWS):
                    p = pb[j, r:r + ROWS, :]
                    cc, rt = r // T, r % T
                    q = None
                    for b in range(0, 256, LN):
                        y1 = yv[r:r + ROWS, b:b + LN] + bd[j, :, c + b:c + b + LN]
                        py[s, cc, rt:rt + ROWS, c + b:c + b + LN] += p * y1
                        t = dyf[r:r + ROWS, c + b:c + b + LN] * y1
                        q = t if q is None else q + t
                    if c == 0:
                        qs[r:r + ROWS, :] = q
                    else:
                        qs[r:r + ROWS, :] += q
            for c in range(0, D, 256):
                dv = lax.dot_general(c_st[par], wgu[j, c:c + 256, :], NT, preferred_element_type=F32)
                pd[s, :, :, c:c + 256] += dv.reshape(2, T, 256)
            sub = lax.broadcasted_iota(jnp.int32, (8, T), 0)
            for cc in range(NC):
                row = col_sum(qs[cc * T:(cc + 1) * T, :].T)
                qt[slot + cc] = jnp.where(sub == j, row, qt[slot + cc])

    def drain(par):
        for cp in st_copies(par, 0, 0):
            cp.wait()

    @pl.loop(0, 4)
    def _(s):
        slot = 2 * s

        @pl.when(s == 0)
        def _():
            ag_wait(7)

        @pl.when(s == 2)
        def _():
            ag_wait(10)

        @pl.when(s + 2 * k == 3)
        def _():
            ag_wait(8)
            ag_wait(9)

        stage_probs(slot)
        py[s] = jnp.zeros((NC, T, D), F32)
        pd[s] = jnp.zeros((NC, T, D), F32)
        qt[slot] = jnp.zeros((8, T), F32)
        qt[slot + 1] = jnp.zeros((8, T), F32)

        @pl.loop(0, EL)
        def _(j):
            it = s * EL + j

            @pl.when(s == 0)
            def _():
                pltpu.make_async_copy(wgu_hbm.at[j], wgu.at[j], w_sem.at[0, j]).wait()
                pltpu.make_async_copy(wdn_hbm.at[j], wdn.at[j], w_sem.at[1, j]).wait()

            @pl.when(it >= 2)
            def _():
                drain(j % 2)

            expert(s, j, slot, True)

            @pl.when((it == 9) & (k == 0))
            def _():
                pair_sum(1, 1)
                pair_sum(2, 0)

            @pl.when(it == 6)
            def _():
                pair_sum(0, 0)
                pair_sum(0, 1)

            @pl.when(it == 12)
            def _():
                pair_sum(3, 0)
                pair_sum(3, 1)

            for cp in st_copies(j % 2, j, slot):
                cp.start()

            @pl.when((it == 1) & (k == 1))
            def _():
                near(1)
                near(2)

            @pl.when((it == 2) & (k == 0))
            def _():
                fetch(1)
                ag_send(2, slot_of(1, k), slot_of(3, k), (d, ep_of(2, k)))
                fetch(2)

            @pl.when((it == 5) & (k == 1))
            def _():
                fetch(2)
                ag_send(2, slot_of(2, k), slot_of(3, k), (d, ep_of(1, k)))
                fetch(1)

            @pl.when(it == 5)
            def _():
                fetch_z(0)

            @pl.when(it == 12 + 3 * k)
            def _():
                fetch_z(1)
                fetch_z(2)

            @pl.when(it == 12)
            def _():
                rs_copy(1).start()
                rs_copy(4).start()

            @pl.when(it == 3)
            def _():
                d2d(0, 0).start()
                d2d(0, 1).start()

            @pl.when(it == 15 - 8 * k)
            def _():
                d2d(1, 0).start()
                d2d(2, 1).start()
                d2d(1, 1).start()
                d2d(2, 0).start()

            @pl.when(it == 11)
            def _():
                d2d(3, 0).start()
                d2d(3, 1).start()

        @pl.when(s == 1)
        def _():
            ag_wait(11)
            stage_probs(8)

            @pl.loop(0, EL)
            def _(j):
                drain(j % 2)
                expert(0, j, 8, False)

                @pl.when((j == 1) & (k == 0))
                def _():
                    pair_sum(1, 0)
                    pair_sum(2, 1)

                for cp in st_copies(j % 2, j, 8):
                    cp.start()

                @pl.when((j == 1) & (k == 0))
                def _():
                    rs_copy(0).start()
                    rs_copy(3).start()

                @pl.when(j == FETCH_D)
                def _():
                    fetch(3)

        for half in range(NC):
            mid = s % 2
            m = mid * (1 + half) + (1 - mid) * (s // 2) * 3
            kk = mid * (s // 2) + (1 - mid) * half

            @pl.when((m > 0) | (kk != k))
            def _():
                q_copy(m, kk).start()

    @pl.loop(1, 4)
    def _(s):
        slot = 8 + 2 * s

        @pl.when(s == 2)
        def _():
            ag_wait(14)

        @pl.when(s + 2 * k == 3)
        def _():
            ag_wait(12)
            ag_wait(13)

        stage_probs(slot)

        @pl.loop(0, EL)
        def _(j):
            it = s * EL + j
            drain(j % 2)
            expert(s, j, slot, False)

            @pl.when((it == 5) & (k == 1))
            def _():
                pair_sum(1, 0)
                pair_sum(2, 1)

            @pl.when((it == 6) & (k == 1))
            def _():
                pair_sum(1, 1)
                pair_sum(2, 0)

            @pl.when(it == MERGE_IT)
            def _():
                rs_copy(1).wait_recv()
                s2, half2 = mine(2)
                py[s2, half2] += ria[:]
                rs_copy(4).wait_recv()
                s1, half1 = mine(1)
                pd[s1, half1] += rib[:]

            for cp in st_copies(j % 2, j, slot):
                cp.start()

            @pl.when((it == 5) & (k == 1))
            def _():
                rs_copy(0).start()
                rs_copy(3).start()

            @pl.when(it == MERGE_IT)
            def _():
                rs_copy(5).start()
                rs_copy(2).start()

            @pl.when(it == 6)
            def _():
                fetch_z(3)

            @pl.when(it == 8)
            def _():
                qbuf[e] = qt[k]
                for i in range(1, 8):
                    pltpu.make_async_remote_copy(qt.at[0], qbuf.at[e], q_s.at[i], q_r.at[i], device_id=sib, device_id_type=MESH).wait_recv()
                q = jnp.concatenate([qbuf[i, :EL, :] for i in range(8)], axis=0)
                prob = pt[k]
                dlog = prob * (q - col_sum(prob * q))
                dlog_s[:] = dlog
                gdl[me] = dlog.astype(BF16)

            @pl.when(it == 9)
            def _():
                @pl.loop(1, 16)
                def _(r):
                    dl_copy(r).start()

    for par in range(NC):
        drain(par)
    for j in range(EL):
        gbgu_ref[j:j + 1, :] = col_sum(accg[j])
        gbdn_ref[j:j + 1, :] = col_sum(accd[j])

    x = x_ref[:].astype(F32)
    inv = lax.rsqrt(row_mean(x * x) + NORM_EPS)
    normed = x * inv
    dlog = dlog_s[:].T
    dhr = jnp.dot(dlog.astype(BF16), wr_ref[:], preferred_element_type=F32)
    for i in (0, 3, 5, 2):
        rs_copy(i).wait_recv()
    d_h = pd[0, k] + rxb[:] + ryb[:] + dhr
    gn = col_sum(d_h * normed)
    for i in range(8):
        ggn[me, i:i + 1, :] = gn[:, i * 128:(i + 1) * 128]
    ggn[me, 8:16, :] = jnp.zeros((8, LN), F32)
    ggn[me, 8:9, :E] = col_sum(dlog)
    y_out[:] = (x + (py[0, k] + rxa[:] + rya[:])).astype(BF16)

    @pl.loop(1, 16)
    def _(r):
        gn_copy(r).start()

    dn = d_h * nw_ref[:].astype(F32).reshape(1, D)
    dt_out[:] = (dout_ref[:].astype(F32) + inv * (dn - normed * row_mean(dn * normed))).astype(BF16)

    for i in range(4):
        for g in range(EL * i, EL * i + EL):
            ht[:, g * T:(g + 1) * T] = hd[g, :, :D].T
        ht_copy(i).start()

    @pl.loop(1, 16)
    def _(r):
        dl_copy(r).wait()

    gr = jnp.zeros((E, D), F32)
    for g in range(16):
        dd, yy, xx, kk = g // 8, g // 4 % 2, g // 2 % 2, g % 2
        slot = 8 * ((dd + d) % 2) + slot_of((xx + cx) % 2 + 2 * ((yy + cy) % 2), kk)
        gr = gr + jnp.dot(gdl[g], hd[slot, :, :D], preferred_element_type=F32)
    gr_out[:] = gr

    for i in range(15):
        for cp in ag_copies(i, 0, 0, sib):
            cp.wait_send()
    for m in range(4):
        d2d(m, 0).wait_send()
        d2d(m, 1).wait_send()
    for i in range(6):
        rs_copy(i).wait_send()
    for i in range(1, 8):
        pltpu.make_async_remote_copy(qt.at[0], qbuf.at[e], q_s.at[i], q_r.at[i], device_id=sib, device_id_type=MESH).wait_send()

    @pl.loop(1, 16)
    def _(r):
        gn_copy(r).wait()

    gn_out[:] = ggn[:]
    for i in range(4):
        ht_copy(i).wait()


def grads_kernel(h_ref, a_ref, c_ref, v_ref, gri_ref, g_ref, yi_ref, ti_ref, bgi_ref, bdi_ref,
                 ggu_ref, gdn_ref, gr_ref, gbr_ref, gn_ref, yo_ref, to_ref, bgo_ref, bdo_ref, at):
    @pl.when((pl.program_id(0) == 0) & (pl.program_id(1) == 0))
    def _():
        gn = jnp.zeros((16, LN), F32)
        for g in range(16):
            gn = gn + g_ref[g]
        gr_ref[:] = gri_ref[:]
        gbr_ref[:] = gn[8:9, :E]
        gn_ref[:] = gn[:8]
        yo_ref[:] = yi_ref[:]
        to_ref[:] = ti_ref[:]
        bgo_ref[:] = bgi_ref[:]
        bdo_ref[:] = bdi_ref[:]

    for g in range(16):
        at[:, g * T:(g + 1) * T] = a_ref[0, g * T:(g + 1) * T, :].T
    ggu_ref[0] = jnp.dot(h_ref[:], c_ref[0], preferred_element_type=F32)
    gdn_ref[0] = jnp.dot(at[:], v_ref[0], preferred_element_type=F32)


def block_body(x_tokens, expert_idx, d_out, norm_w, w_router, b_router, w_gate_up, b_gate_up, w_down, b_down):
    vm = pl.BlockSpec(memory_space=pltpu.VMEM)
    hb = pl.BlockSpec(memory_space=pl.ANY)
    s = jax.ShapeDtypeStruct
    dma = pltpu.SemaphoreType.DMA
    out = pl.pallas_call(
        block_kernel,
        out_shape=(s((T, D), BF16), s((T, D), BF16), s((EL, D), F32), s((EL, D), F32), s((E, D), F32), s((16, 16, LN), F32),
                   s((D, N), BF16), s((EL, N, F), BF16), s((EL, N, FF), BF16), s((EL, N, D), BF16)),
        in_specs=[vm, vm, vm, vm, vm, vm, hb, vm, hb, vm],
        out_specs=(vm, vm, vm, vm, vm, vm, hb, hb, hb, hb),
        scratch_shapes=[
            pltpu.VMEM((16, T, 2 * D), BF16),
            pltpu.VMEM((16, E, T), F32),
            pltpu.VMEM((EL, TT, LN), F32),
            pltpu.VMEM((EL, D, FF), BF16),
            pltpu.VMEM((EL, F, D), BF16),
            pltpu.VMEM((TT, FF), F32),
            pltpu.VMEM((TT, F), F32),
            pltpu.VMEM((2, TT, F), BF16),
            pltpu.VMEM((2, TT, FF), BF16),
            pltpu.VMEM((2, TT, D), BF16),
            pltpu.VMEM((TT, D), F32),
            pltpu.VMEM((TT, LN), F32),
            pltpu.VMEM((EL, 1, FF), F32),
            pltpu.VMEM((EL, 1, D), F32),
            pltpu.VMEM((4, 2, T, D), F32),
            pltpu.VMEM((4, 2, T, D), F32),
            pltpu.VMEM((4, T, D), F32),
            pltpu.VMEM((4, T, D), F32),
        ] + [pltpu.VMEM((T, D), F32)] * 6 + [
            pltpu.VMEM((8, 8, T), F32),
            pltpu.VMEM((8, 8, T), F32),
            pltpu.VMEM((E, T), F32),
            pltpu.VMEM((16, E, T), BF16),
            pltpu.VMEM((16, 16, LN), F32),
            pltpu.VMEM((D, N), BF16),
            pltpu.VMEM((EL, 8, FF), F32),
            pltpu.VMEM((EL, 8, D), F32),
        ] + [dma((15,))] * 4 + [dma((8,))] * 2 + [dma((6,))] * 2 + [dma((8,))] * 2 + [dma((16,))] * 4 + [
            dma((2, EL)), dma((3, 2)), dma((4,)),
        ],
        compiler_params=pltpu.CompilerParams(collective_id=0, has_side_effects=True, vmem_limit_bytes=62 * 1024 * 1024),
        name="moe_block",
    )(x_tokens, expert_idx.T, d_out, norm_w, w_router.T, b_router, w_gate_up, b_gate_up, w_down, b_down)
    y_out, d_tok, gb_gu, gb_dn, g_r, gn_all, h_all, a_all, c_all, v_all = out
    half = D // 2

    def full(shape):
        return pl.BlockSpec(shape, lambda j, t: (0,) * len(shape))

    g_gu, g_dn, g_r, g_br, g_n, y_out, d_tok, gb_gu, gb_dn = pl.pallas_call(
        grads_kernel,
        grid=(EL, 2),
        out_shape=(s((EL, D, FF), F32), s((EL, F, D), F32), s((E, D), F32), s((1, E), F32), s((8, LN), F32),
                   s((T, D), BF16), s((T, D), BF16), s((EL, D), F32), s((EL, D), F32)),
        in_specs=[
            full((D, N)),
            pl.BlockSpec((1, N, F), lambda j, t: (j, 0, 0)),
            pl.BlockSpec((1, N, half), lambda j, t: (j, 0, t)),
            pl.BlockSpec((1, N, half), lambda j, t: (j, 0, t)),
            full((E, D)), full((16, 16, LN)), full((T, D)), full((T, D)), full((EL, D)), full((EL, D)),
        ],
        out_specs=(
            pl.BlockSpec((1, D, half), lambda j, t: (j, 0, t)),
            pl.BlockSpec((1, F, half), lambda j, t: (j, 0, t)),
            full((E, D)), full((1, E)), full((8, LN)), full((T, D)), full((T, D)), full((EL, D)), full((EL, D)),
        ),
        scratch_shapes=[pltpu.VMEM((F, N), BF16)],
        compiler_params=pltpu.CompilerParams(dimension_semantics=("arbitrary", "arbitrary"), vmem_limit_bytes=60 * 1024 * 1024),
        name="weight_grads",
    )(h_all, a_all, c_all, v_all, g_r, gn_all, y_out, d_tok, gb_gu, gb_dn)
    return (y_out, d_tok, g_gu, gb_gu, g_dn, gb_dn, g_r.T, g_br.reshape(E), g_n.reshape(D))


def solution(mesh):
    tok = P(("dp", "ep"), None)
    w3 = P("ep", None, None)
    w2 = P("ep", None)
    in_specs = (tok, tok, tok, P(), P(), P(), w3, w2, w3, w2)
    out_specs = (tok, tok, w3, w2, w3, w2, P(), P(), P())
    return jax.shard_map(block_body, mesh=mesh, in_specs=in_specs, out_specs=out_specs, check_vma=False)
```

time: 139 us -> 121 us (0.87)
  Pallas kernels: 138 us -> 120 us
    pallas_call x1, Pallas kernels: 102 us -> 85.3 us  [block_body(): pl.pallas_call(block_kernel, out_shape=(s((T, D), BF16), s((T, D), BF16),...]
where the time goes in v3:
time: 121 us
  Pallas kernels  120 us (99%)
    pallas_call x1, Pallas kernels, block_body(): pl.pallas_call(block_kernel, out_shape=(s((T, D), BF16), s((T, D), BF16),...  85.3 us
    pallas_call x1, Pallas kernels, block_body(): pl.pallas_call(grads_kernel, grid=(EL, 2), out_shape=(s((EL, D, FF), F32)...  34.7 us

profile of v3, /device:TPU:0, one launch (start us, length us, event | category | flops | bytes accessed | tf_op | source)
XLA Modules:
  0.0 120.7 jit_solution(16539310784602686449)
XLA Ops:
  0.6 85.3 %moe_block.1 = (bf16[128,1024]{1,0:T(8,128)(2,1)}, bf16[128,1024]{1,0:T(8,128)(2,1)}, f32[4,1024]{1,0:T(4,128)}, f32[4,1024]{1,0:T(4,128)}, f32[32,1024]{1,0:T(8...) custom-call(bf16[128,1024]{1,0:T(8,128)(2,1)} %x_ref.1, ...), custom_call_target="tpu_custom_call" | custom-call | tf_op jit(solution)/shard_map/moe_block/pallas_call | solution.py:564
  86.0 34.7 %weight_grads.1 = (f32[4,1024,1024]{2,1,0:T(8,128)}, f32[4,512,1024]{2,1,0:T(8,128)}, f32[32,1024]{1,0:T(8,128)}, f32[1,32]{1,0:T(1,128)}, f32[8,128]{1,0:T(8,12...) custom-call(bf16[1024,2048]{1,0:T(8,128)(2,1)} %get-tuple-element.28.h_ref, ...), custom_call_target="tpu_custom_call" | custom-call | tf_op jit(solution)/shard_map/weight_grads/pallas_call | solution.py:610
